TPU v7x, 32 devices: a whole 2x2x4 slice. The times are simulated.
32 devices in a mesh: grp: 2 (over x), comp: 4 (over z), row: 4 (over y, core).
Axes of the slice: x: 2, y: 2, z: 4, core: 2. Of those that a mesh axis runs over, the one named last changes fastest.
Arguments:
- points: bfloat16 [16384, 1024], P(('grp', 'row')), parts along dimension 0
- mu_init: float32 [2, 2048, 512], P(None, ('grp', 'comp')), parts along dimension 1
- logpi_init: float32 [2, 2048], P(None, ('grp', 'comp')), parts along dimension 1
- inv_temp: float32 [3], replicated
Outputs:
- output 1: float32 [2, 2048, 512], P(None, ('grp', 'comp')), parts along dimension 1
- output 2: float32 [2, 2048], P(None, ('grp', 'comp')), parts along dimension 1
- output 3: float32 [2, 16384], P(None, ('grp', 'row')), parts along dimension 1
There are 2 independent parts. A program takes and returns all parts, laid end to end along the dimension named above; an argument that names none is the same for every part.
All inputs are finite; a program needn't handle non-finite values.
Results may differ from a plain program's by a relative error of at most 0.001.
Values are sent between devices in bfloat16 or wider.
A program may use at most 1 GiB of HBM per device.

v0:
```python
import jax
import jax.numpy as jnp
from jax import lax
from jax.sharding import PartitionSpec as P

EPS_COUNT = 1e-6
PRIOR_ALPHA = 1e-3


def solution(mesh):
    comp_size = mesh.shape["comp"]
    row_size = mesh.shape["row"]

    def local_fit(x_local, mu_init, logpi_init, inv_temp):
        n_rows, full_dim = x_local.shape
        half_dim = full_dim // 2
        n_local = mu_init.shape[1]
        total_pts = n_rows * row_size
        total_comp = n_local * comp_size
        x_fits = jnp.transpose(x_local.reshape(n_rows, 2, half_dim), (1, 0, 2))
        sq_norm = jnp.sum(jnp.square(x_fits.astype(jnp.float32)), axis=2)
        mean_vecs = mu_init
        log_wts = logpi_init
        for sweep_idx in range(inv_temp.shape[0]):
            beta_t = inv_temp[sweep_idx]
            mu_sq = jnp.sum(mean_vecs * mean_vecs, axis=2)
            cross_dot = jnp.einsum("snh,skh->snk", x_fits, mean_vecs.astype(jnp.bfloat16), preferred_element_type=jnp.float32)
            logits = log_wts[:, None, :] - beta_t * (sq_norm[:, :, None] - 2.0 * cross_dot + mu_sq[:, None, :])
            row_max = lax.pmax(jnp.max(logits, axis=2), "comp")
            shifted = jnp.exp(logits - row_max[:, :, None])
            row_sum = lax.psum(jnp.sum(shifted, axis=2), "comp")
            log_norm = row_max + jnp.log(row_sum)
            resp_f = shifted / row_sum[:, :, None]
            counts = jnp.sum(resp_f, axis=1)
            stat_sum = jnp.einsum("snk,snh->skh", resp_f.astype(jnp.bfloat16), x_fits, preferred_element_type=jnp.float32)
            counts, stat_sum = lax.psum((counts, stat_sum), "row")
            mean_vecs = stat_sum / (counts[:, :, None] + EPS_COUNT)
            log_wts = jnp.log((counts + PRIOR_ALPHA) / (total_pts + total_comp * PRIOR_ALPHA))
        return mean_vecs, log_wts, log_norm

    return jax.shard_map(
        local_fit,
        mesh=mesh,
        in_specs=(P(("grp", "row"), None), P(None, ("grp", "comp"), None), P(None, ("grp", "comp")), P()),
        out_specs=(P(None, ("grp", "comp"), None), P(None, ("grp", "comp")), P(None, ("grp", "row"))),
        check_vma=False,
    )
```

profile of v0, /device:TPU:0, one launch (start us, length us, event | category | flops | bytes accessed | tf_op | source)
XLA Modules:
  0.0 284.3 jit_solution(7900277503071534673)
XLA Ops:
  7.2 0.0 copy-start.2
  7.2 0.0 copy-start.3
  7.2 0.0 all-reduce.4.cloned.1.call-start
  7.2 0.0 copy-start.1
  7.2 1.5 fusion.32
  8.7 1.5 multiply_reduce_fusion.3
  10.2 3.1 %multiply_reduce_fusion = f32[2,2048]{1,0:T(2,128)S(1)} fusion(bf16[256,2,8,512]{3,2,1,0:T(8,128)(2,1)} %bitcast.76), kind=kLoop, calls=%fused_computation | loop fusion | flops 6287360 | bytes 4210688 | tf_op jit(solution)/shard_map/reduce_sum | solution.py:21
  13.3 0.0 copy-done.2
  13.3 0.0 copy-done.3
  13.3 0.0 copy-done.1
  13.3 3.8 %fusion.33 = (f32[2,2048]{1,0:T(2,128)S(1)}, f32[2,2048,256]{1,2,0:T(8,128)}) fusion(f32[2,256]{1,0:T(2,128)S(1)} %multiply_reduce_fusion.3, f32[2,256,512]{2,1,0:T(8,128)S(1)} %copy-done.2, bf16[256,2,8,512]{3,2,1,0:T(8,128)(2,1)S(1)} %bitcast.82, f32[2,2048]{1,0:T(2,128)S(1)} %multiply_reduce_fusion, f32[]{:T(128)} %bitcast, f32[2,256]{1,0:T(2,128)S(1)} %copy-done.3), kind=kOutput, calls=%fused_computation.53 | convolution fusion | flops 1080291328 | bytes 9474052 | tf_op jit(solution)/shard_map/snh,skh->snk/dot_general | solution.py:27
  17.1 20.5 %pmax.21 = f32[2,2048]{1,0:T(2,128)S(1)} all-reduce(f32[2,2048]{1,0:T(2,128)S(1)} %get-tuple-element.12), channel_id=1, replica_groups=mesh['grp'=2,'comp'=4,'row'=4] {'comp'}, use_global_device_ids=true, to_apply=%region_3.0 | all-reduce | flops 4096 | bytes 32768 | tf_op jit(solution)/shard_map/pmax | solution.py:29
  37.6 2.8 fusion.9
  40.4 15.5 %psum.63 = f32[2,2048]{1,0:T(2,128)S(1)} all-reduce(f32[2,2048]{1,0:T(2,128)S(1)} %fusion.9), channel_id=1, replica_groups=mesh['grp'=2,'comp'=4,'row'=4] {'comp'}, use_global_device_ids=true, to_apply=%region_5.0 | all-reduce | flops 4096 | bytes 32768 | tf_op jit(solution)/shard_map/psum | solution.py:31
  55.9 5.7 %fusion.4 = f32[2,256,512]{2,1,0:T(8,128)} fusion(bf16[256,2,8,512]{3,2,1,0:T(8,128)(2,1)} %bitcast.77, f32[2,2048,256]{1,2,0:T(8,128)} %get-tuple-element.13, f32[2,2048]{1,0:T(2,128)S(1)} %psum.63, f32[2,2048]{1,0:T(2,128)S(1)} %pmax.21), kind=kOutput, calls=%fused_computation.6 | convolution fusion | flops 1076887552 | bytes 9469952 | tf_op jit(solution)/shard_map/snk,snh->skh/dot_general | solution.py:35
  61.6 0.0 all-reduce.4.cloned.1.call-update
  61.7 0.0 all-reduce.6.cloned.1.call-start
  61.7 3.0 %fusion.28 = f32[2,256]{1,0:T(2,128)S(1)} fusion(f32[2,2048]{1,0:T(2,128)S(1)} %psum.63, f32[2,2048,256]{1,2,0:T(8,128)} %get-tuple-element.13, f32[2,2048]{1,0:T(2,128)S(1)} %pmax.21), kind=kLoop, calls=%fused_computation.35 | loop fusion | flops 3145216 | bytes 4229120 | tf_op jit(solution)/shard_map/reduce_sum | solution.py:34
  64.7 6.2 %psum.64 = f32[2,256]{1,0:T(2,128)S(1)} all-reduce(f32[2,256]{1,0:T(2,128)S(1)} %fusion.28), channel_id=1, replica_groups=mesh['grp'=2,'comp'=4,'row'=4] {'row'}, use_global_device_ids=true, to_apply=%region_7.0 | all-reduce | flops 512 | bytes 4096 | tf_op jit(solution)/shard_map/psum | solution.py:36
  70.9 25.8 %all-reduce.4.cloned.1.call-done = f32[2,256,512]{2,1,0:T(8,128)} async-done(((f32[2,256,512]{2,1,0:T(8,128)}), f32[2,256,512]{2,1,0:T(8,128)}) %all-reduce.4.cloned.1.call-update) | async-done | bytes 1048592 | tf_op jit(solution)/shard_map/psum | solution.py:36
  96.7 1.5 multiply_reduce_fusion.2
  98.2 6.8 %bitcast_reduce_fusion.1 = (f32[2,2048]{1,0:T(2,128)S(1)}, f32[2,256,2048]{2,1,0:T(8,128)}) fusion(f32[2,256]{1,0:T(2,128)S(1)} %multiply_reduce_fusion.2, bf16[256,2,8,512]{3,2,1,0:T(8,128)(2,1)} %bitcast.78, f32[2,256,512]{2,1,0:T(8,128)} %all-reduce.4.cloned.1.call-done, f32[2,256]{1,0:T(2,128)S(1)} %get-tuple-element.7, ...), kind=kOutput, calls=%fused_computation.12 | convolution fusion | flops 1080553472 | bytes 9476100 | tf_op jit(solution)/shard_map/snh,skh->snk/dot_general | solution.py:27
  105.0 18.7 %pmax.22 = f32[2,2048]{1,0:T(2,128)S(1)} all-reduce(f32[2,2048]{1,0:T(2,128)S(1)} %get-tuple-element.14), channel_id=1, replica_groups=mesh['grp'=2,'comp'=4,'row'=4] {'comp'}, use_global_device_ids=true, to_apply=%region_11.0 | all-reduce | flops 4096 | bytes 32768 | tf_op jit(solution)/shard_map/pmax | solution.py:29
  123.8 2.8 fusion.11
  126.5 15.6 %psum.66 = f32[2,2048]{1,0:T(2,128)S(1)} all-reduce(f32[2,2048]{1,0:T(2,128)S(1)} %fusion.11), channel_id=1, replica_groups=mesh['grp'=2,'comp'=4,'row'=4] {'comp'}, use_global_device_ids=true, to_apply=%region_13.0 | all-reduce | flops 4096 | bytes 32768 | tf_op jit(solution)/shard_map/psum | solution.py:31
  142.1 5.7 %fusion.2 = f32[2,256,512]{2,1,0:T(8,128)} fusion(bf16[256,2,8,512]{3,2,1,0:T(8,128)(2,1)} %bitcast.79, f32[2,256,2048]{2,1,0:T(8,128)} %get-tuple-element.15, f32[2,2048]{1,0:T(2,128)S(1)} %psum.66, f32[2,2048]{1,0:T(2,128)S(1)} %pmax.22), kind=kOutput, calls=%fused_computation.4 | convolution fusion | flops 1076887552 | bytes 9469952 | tf_op jit(solution)/shard_map/snk,snh->skh/dot_general | solution.py:35
  147.8 0.0 all-reduce.6.cloned.1.call-update
  147.8 0.0 all-reduce.8.cloned.1.call-start
  147.9 3.0 %fusion.26 = f32[2,256]{1,0:T(2,128)S(1)} fusion(f32[2,2048]{1,0:T(2,128)S(1)} %psum.66, f32[2,2048]{1,0:T(2,128)S(1)} %pmax.22, f32[2,256,2048]{2,1,0:T(8,128)} %get-tuple-element.15), kind=kLoop, calls=%fused_computation.34 | loop fusion | flops 3145216 | bytes 4229120 | tf_op jit(solution)/shard_map/reduce_sum | solution.py:34
  150.8 6.4 %psum.67 = f32[2,256]{1,0:T(2,128)S(1)} all-reduce(f32[2,256]{1,0:T(2,128)S(1)} %fusion.26), channel_id=1, replica_groups=mesh['grp'=2,'comp'=4,'row'=4] {'row'}, use_global_device_ids=true, to_apply=%region_15.0 | all-reduce | flops 512 | bytes 4096 | tf_op jit(solution)/shard_map/psum | solution.py:36
  157.2 24.9 %all-reduce.6.cloned.1.call-done = f32[2,256,512]{2,1,0:T(8,128)} async-done(((f32[2,256,512]{2,1,0:T(8,128)}), f32[2,256,512]{2,1,0:T(8,128)}) %all-reduce.6.cloned.1.call-update) | async-done | bytes 1048592 | tf_op jit(solution)/shard_map/psum | solution.py:36
  182.1 1.5 multiply_reduce_fusion.1
  183.6 6.8 %bitcast_reduce_fusion = (f32[2,2048]{1,0:T(2,128)S(1)}, f32[2,256,2048]{2,1,0:T(8,128)}) fusion(f32[2,256]{1,0:T(2,128)S(1)} %multiply_reduce_fusion.1, bf16[256,2,8,512]{3,2,1,0:T(8,128)(2,1)} %bitcast.80, f32[2,256,512]{2,1,0:T(8,128)} %all-reduce.6.cloned.1.call-done, f32[2,256]{1,0:T(2,128)S(1)} %get-tuple-element.5, ...), kind=kOutput, calls=%fused_computation.9 | convolution fusion | flops 1080553472 | bytes 9476100 | tf_op jit(solution)/shard_map/snh,skh->snk/dot_general | solution.py:27
  190.5 18.7 %pmax.23 = f32[2,2048]{1,0:T(2,128)S(1)} all-reduce(f32[2,2048]{1,0:T(2,128)S(1)} %get-tuple-element.16), channel_id=1, replica_groups=mesh['grp'=2,'comp'=4,'row'=4] {'comp'}, use_global_device_ids=true, to_apply=%region_19.0 | all-reduce | flops 4096 | bytes 32768 | tf_op jit(solution)/shard_map/pmax | solution.py:29
  209.2 2.8 fusion.13
  211.9 15.6 %psum.69 = f32[2,2048]{1,0:T(2,128)S(1)} all-reduce(f32[2,2048]{1,0:T(2,128)S(1)} %fusion.13), channel_id=1, replica_groups=mesh['grp'=2,'comp'=4,'row'=4] {'comp'}, use_global_device_ids=true, to_apply=%region_21.0 | all-reduce | flops 4096 | bytes 32768 | tf_op jit(solution)/shard_map/psum | solution.py:31
  227.5 0.0 copy-start
  227.5 3.1 %fusion.23 = f32[2,256]{1,0:T(2,128)S(1)} fusion(f32[2,2048]{1,0:T(2,128)S(1)} %psum.69, f32[2,2048]{1,0:T(2,128)S(1)} %pmax.23, f32[2,256,2048]{2,1,0:T(8,128)} %get-tuple-element.17), kind=kLoop, calls=%fused_computation.33 | loop fusion | flops 3145216 | bytes 4229120 | tf_op jit(solution)/shard_map/reduce_sum | solution.py:34
  230.6 0.3 copy-done
  231.0 4.5 %fusion = f32[2,256,512]{2,1,0:T(8,128)} fusion(bf16[256,2,8,512]{3,2,1,0:T(8,128)(2,1)} %bitcast.81, f32[2,256,2048]{2,1,0:T(8,128)S(1)} %copy-done, f32[2,2048]{1,0:T(2,128)S(1)} %psum.69, f32[2,2048]{1,0:T(2,128)S(1)} %pmax.23), kind=kOutput, calls=%fused_computation.2 | convolution fusion | flops 1076887552 | bytes 9469952 | tf_op jit(solution)/shard_map/snk,snh->skh/dot_general | solution.py:35
  235.5 5.6 %psum.71 = f32[2,256]{1,0:T(2,128)S(1)} all-reduce(f32[2,256]{1,0:T(2,128)S(1)} %fusion.23), channel_id=1, replica_groups=mesh['grp'=2,'comp'=4,'row'=4] {'row'}, use_global_device_ids=true, to_apply=%region_24.0 | all-reduce | flops 512 | bytes 4096 | tf_op jit(solution)/shard_map/psum | solution.py:36
  241.1 0.0 all-reduce.8.cloned.1.call-update
  241.1 0.6 multiply_log_fusion
  241.7 0.6 log_add_fusion
  242.4 33.1 %all-reduce.8.cloned.1.call-done = f32[2,256,512]{2,1,0:T(8,128)} async-done(((f32[2,256,512]{2,1,0:T(8,128)}), f32[2,256,512]{2,1,0:T(8,128)}) %all-reduce.8.cloned.1.call-update) | async-done | bytes 1048592 | tf_op jit(solution)/shard_map/psum | solution.py:36
  275.5 2.3 broadcast_divide_fusion
  (2 shorter events, 0.0 us)
Async XLA Ops:
  7.2 6.1 %copy-start.2 = (f32[2,256,512]{2,1,0:T(8,128)S(1)}, f32[2,256,512]{2,1,0:T(8,128)}, u32[]{:S(2)}) copy-start(f32[2,256,512]{2,1,0:T(8,128)} %param.5) | copy-start | bytes 3145732
  7.2 6.1 %copy-start.3 = (f32[2,256]{1,0:T(2,128)S(1)}, f32[2,256]{1,0:T(2,128)}, u32[]{:S(2)}) copy-start(f32[2,256]{1,0:T(2,128)} %param.6) | copy-start | bytes 6148
  7.2 89.6 %all-reduce.4.cloned.1.call-start = ((), (), s32[]{:S(2)}) async-start(), calls=%async_computation | async-start | bytes 2097152 | tf_op jit(solution)/shard_map/psum | solution.py:36
  7.2 6.1 %copy-start.1 = (bf16[2048,1024]{1,0:T(8,128)(2,1)S(1)}, bf16[2048,1024]{1,0:T(8,128)(2,1)}, u32[]{:S(2)}) copy-start(bf16[2048,1024]{1,0:T(8,128)(2,1)} %param.4) | copy-start | bytes 12582916
  61.7 120.5 %all-reduce.6.cloned.1.call-start = ((), (), s32[]{:S(2)}) async-start(), calls=%async_computation.1 | async-start | bytes 2097152 | tf_op jit(solution)/shard_map/psum | solution.py:36
  147.8 127.6 %all-reduce.8.cloned.1.call-start = ((), (), s32[]{:S(2)}) async-start(), calls=%async_computation.2 | async-start | bytes 2097152 | tf_op jit(solution)/shard_map/psum | solution.py:36
  227.5 3.4 %copy-start = (f32[2,256,2048]{2,1,0:T(8,128)S(1)}, f32[2,256,2048]{2,1,0:T(8,128)}, u32[]{:S(2)}) copy-start(f32[2,256,2048]{2,1,0:T(8,128)} %get-tuple-element.17) | copy-start | bytes 12582916
Sparse Core Ops, SparseCore 0:
  61.8 34.9 all-reduce.3
  148.0 34.1 all-reduce.5
  241.3 34.1 all-reduce.7
where the time goes:
time: 285 us; the launch traced here: 284 us
  blocking collectives  123 us (43%)
  waiting for transfers between devices  83.9 us (29%)
  matrix products  33.3 us (12%)
  other arithmetic  28.4 us (10%)
  between operations  13.8 us (5%)
    psum x3, waiting for transfers between devices, local_fit(): counts, stat_sum = lax.psum((counts, stat_sum), 'row')  83.8 us
    pmax x3, blocking collectives, local_fit(): row_max = lax.pmax(jnp.max(logits, axis=2), 'comp')  57.9 us
    psum x3, blocking collectives, local_fit(): row_sum = lax.psum(jnp.sum(shifted, axis=2), 'comp')  46.7 us
    psum x3, blocking collectives, local_fit(): counts, stat_sum = lax.psum((counts, stat_sum), 'row')  18.2 us
    dot_general x3, matrix products, local_fit(): jnp.einsum('snh,skh->snk', x_fits, mean_vecs.astype(jnp.bfloat16), prefer...  17.5 us
    dot_general x3, matrix products, local_fit(): jnp.einsum('snk,snh->skh', resp_f.astype(jnp.bfloat16), x_fits, preferred...  15.9 us
    reduce_sum x3, other arithmetic, local_fit(): counts = jnp.sum(resp_f, axis=1)  9.01 us
    reduce_sum x3, other arithmetic, local_fit(): row_sum = lax.psum(jnp.sum(shifted, axis=2), 'comp')  8.32 us
  transfers between devices with their start and end apart: 3, of which 3 were waited for; matrix products, arithmetic and copies ran while one was open for 3% of the time, Pallas kernels for 0%

commit v1 on v0

v1 whole, which is shorter than its diff:
```python
import functools

import jax
import jax.numpy as jnp
from jax import lax
from jax.experimental import pallas as pl
from jax.experimental.pallas import tpu as pltpu
from jax.sharding import PartitionSpec as P

EPS_COUNT = 1e-6
PRIOR_ALPHA = 1e-3
MESH = pl.DeviceIdType.MESH
LANE_BLOCK = 256
N_CHUNKS = 4


def _col(row):
    n = row.shape[1]
    parts = [
        jnp.transpose(jnp.broadcast_to(row[:, i : i + 128], (128, 128)))
        for i in range(0, n, 128)
    ]
    return parts[0] if len(parts) == 1 else jnp.concatenate(parts, axis=0)


def _lane_sum_row(block):
    n = block.shape[0]
    parts = [
        jnp.sum(jnp.transpose(block[i : i + 128, :]), axis=0, keepdims=True)
        for i in range(0, n, 128)
    ]
    return parts[0] if len(parts) == 1 else jnp.concatenate(parts, axis=1)


def _fold(x):
    acc = x[:, 0:128]
    for i in range(128, x.shape[1], 128):
        acc = acc + x[:, i : i + 128]
    return acc


def em_kernel(
    n_z, n_sweeps, log_denom,
    x_hbm, mu_hbm, lp_ref, beta_ref,
    mu_out, lp_out, lse_out,
    x_v, mu_f, mu_b, p_v, r_v, s_v, s_rx, s_rx_last, n_tx, n_rx, c_tx, c_rx,
    z_tx, z_rx, m_v, sqx_v, lse_v, lse_rx, lp_rx,
    ld_sem, xs_sem, xr_sem, zs_sem, zr_sem, ss_sem, sr_sem, ns_sem, nr_sem,
    as_sem, ar_sem, cs_sem, cr_sem, ls_sem, lr_sem, os_sem, or_sem,
):
    row = lax.axis_index("row")
    zz = lax.axis_index("comp")
    core = lax.rem(row, 2)
    yy = lax.div(row, 2)
    fit = core
    other = 1 - core
    y_peer = {"row": (1 - yy) * 2 + core}
    c_peer = {"row": yy * 2 + (1 - core)}
    z_peers = [{"comp": lax.rem(zz + d, n_z)} for d in range(1, n_z)]

    n_rows = x_v.shape[0]
    own_rows = n_rows // 2
    k_dim, h_dim = mu_f.shape
    k_half = k_dim // 2
    chunk = n_rows // N_CHUNKS
    per_chunk = chunk // LANE_BLOCK
    mine = pl.multiple_of(yy * k_half, k_half)
    theirs = pl.multiple_of((1 - yy) * k_half, k_half)
    own_chunks = N_CHUNKS // 2

    loads = []
    mu_load = pltpu.make_async_copy(mu_hbm.at[fit], mu_f, ld_sem.at[0])
    mu_load.start()
    for i in range(own_chunks):
        cp = pltpu.make_async_copy(
            x_hbm.at[pl.ds(i * chunk, chunk), pl.ds(pl.multiple_of(fit * h_dim, h_dim), h_dim)],
            x_v.at[pl.ds(i * chunk, chunk)],
            ld_sem.at[1 + i],
        )
        cp.start()
        loads.append(cp)

    barrier = pltpu.get_barrier_semaphore()
    for peer in [c_peer, y_peer] + z_peers:
        pl.semaphore_signal(barrier, inc=1, device_id=peer, device_id_type=MESH)
    pl.semaphore_wait(barrier, 1 + n_z)

    swaps = []
    for i in range(own_chunks):
        cp = pltpu.make_async_remote_copy(
            src_ref=x_hbm.at[pl.ds(i * chunk, chunk), pl.ds(pl.multiple_of(other * h_dim, h_dim), h_dim)],
            dst_ref=x_v.at[pl.ds(own_rows + i * chunk, chunk)],
            send_sem=xs_sem.at[i],
            recv_sem=xr_sem.at[i],
            device_id=c_peer,
            device_id_type=MESH,
        )
        cp.start()
        swaps.append(cp)

    mu_load.wait()
    mu0 = mu_f[...]
    mu_b[...] = mu0.astype(jnp.bfloat16)
    lp0 = jnp.where(core == 0, lp_ref[0:1, :], lp_ref[1:2, :])
    c_row = lp0 - beta_ref[0] * _lane_sum_row(_fold(mu0 * mu0))
    c_col = _col(c_row)

    for t in range(n_sweeps):
        last = t == n_sweeps - 1
        beta = beta_ref[t]
        z_copies = []
        for ci in range(N_CHUNKS):
            if t == 0:
                if ci < own_chunks:
                    loads[ci].wait()
                else:
                    swaps[ci - own_chunks].wait_recv()
            for bi in range(per_chunk):
                r0 = ci * chunk + bi * LANE_BLOCK
                a = lax.dot_general(
                    mu_b[...], x_v[r0 : r0 + LANE_BLOCK, :],
                    (((1,), (1,)), ((), ())), preferred_element_type=jnp.float32,
                )
                lg = a * (2.0 * beta) + jnp.concatenate([c_col] * (LANE_BLOCK // 128), axis=1)
                m = jnp.max(lg, axis=0, keepdims=True)
                p = jnp.exp(lg - m)
                l = m + jnp.log(jnp.sum(p, axis=0, keepdims=True))
                p_v[:, r0 : r0 + LANE_BLOCK] = p
                m_v[:, r0 : r0 + LANE_BLOCK] = m
                z_tx[t, ci, :, bi * LANE_BLOCK : (bi + 1) * LANE_BLOCK] = l
            copies = []
            for d, peer in enumerate(z_peers):
                cp = pltpu.make_async_remote_copy(
                    src_ref=z_tx.at[t, ci],
                    dst_ref=z_rx.at[t, ci, d],
                    send_sem=zs_sem.at[t, ci, d],
                    recv_sem=zr_sem.at[t, ci, d],
                    device_id=peer,
                    device_id_type=MESH,
                )
                cp.start()
                copies.append(cp)
            z_copies.append(copies)

        n_acc = jnp.zeros((k_dim, 128), jnp.float32)
        for ci in range(N_CHUNKS):
            for cp in z_copies[ci]:
                cp.wait_recv()
            for bi in range(per_chunk):
                r0 = ci * chunk + bi * LANE_BLOCK
                sl = slice(bi * LANE_BLOCK, (bi + 1) * LANE_BLOCK)
                parts = [z_tx[t, ci, :, sl]] + [z_rx[t, ci, d, :, sl] for d in range(n_z - 1)]
                top = functools.reduce(jnp.maximum, parts)
                tot = functools.reduce(lambda u, v: u + v, [jnp.exp(q - top) for q in parts])
                lse = top + jnp.log(tot)
                scale = jnp.exp(m_v[:, r0 : r0 + LANE_BLOCK] - lse)
                r = p_v[:, r0 : r0 + LANE_BLOCK] * scale
                r_v[:, r0 : r0 + LANE_BLOCK] = r.astype(jnp.bfloat16)
                n_acc = n_acc + _fold(r)
                if last:
                    lse_v[:, r0 : r0 + LANE_BLOCK] = lse - beta * sqx_v[:, r0 : r0 + LANE_BLOCK]
        n_part = _lane_sum_row(n_acc)
        n_tx[t] = n_part
        n_copy = pltpu.make_async_remote_copy(
            src_ref=n_tx.at[t], dst_ref=n_rx.at[t], send_sem=ns_sem.at[t], recv_sem=nr_sem.at[t],
            device_id=y_peer, device_id_type=MESH,
        )
        n_copy.start()

        s_copies = []
        for hi in range(2):
            cols = slice(hi * (h_dim // 2), (hi + 1) * (h_dim // 2))
            s_v[pl.ds(theirs, k_half), cols] = jnp.dot(
                r_v[pl.ds(theirs, k_half), :], x_v[:, cols], preferred_element_type=jnp.float32
            )
            dst = s_rx_last.at[pl.ds(theirs, k_half), cols] if last else s_rx.at[t, :, cols]
            cp = pltpu.make_async_remote_copy(
                src_ref=s_v.at[pl.ds(theirs, k_half), cols], dst_ref=dst,
                send_sem=ss_sem.at[t, hi], recv_sem=sr_sem.at[t, hi],
                device_id=y_peer, device_id_type=MESH,
            )
            cp.start()
            s_copies.append(cp)
        for hi in range(2):
            cols = slice(hi * (h_dim // 2), (hi + 1) * (h_dim // 2))
            s_v[pl.ds(mine, k_half), cols] = jnp.dot(
                r_v[pl.ds(mine, k_half), :], x_v[:, cols], preferred_element_type=jnp.float32
            )
            if last:
                cp = pltpu.make_async_remote_copy(
                    src_ref=s_v.at[pl.ds(mine, k_half), cols],
                    dst_ref=s_rx_last.at[pl.ds(mine, k_half), cols],
                    send_sem=ss_sem.at[t, 2 + hi], recv_sem=sr_sem.at[t, 2 + hi],
                    device_id=y_peer, device_id_type=MESH,
                )
                cp.start()
                s_copies.append(cp)

        if t == 0:
            ones = jnp.ones((16, h_dim), jnp.bfloat16)
            for b in range(n_rows // LANE_BLOCK):
                r0 = b * LANE_BLOCK
                xf = x_v[r0 : r0 + LANE_BLOCK, :].astype(jnp.float32)
                sq = xf * xf
                hi_part = sq.astype(jnp.bfloat16)
                lo_part = (sq - hi_part.astype(jnp.float32)).astype(jnp.bfloat16)
                acc = lax.dot_general(ones, hi_part, (((1,), (1,)), ((), ())), preferred_element_type=jnp.float32)
                acc = acc + lax.dot_general(ones, lo_part, (((1,), (1,)), ((), ())), preferred_element_type=jnp.float32)
                sqx_v[:, r0 : r0 + LANE_BLOCK] = acc[0:1, :]

        if not last:
            n_copy.wait_recv()
            n_all = n_part + n_rx[t]
            n_own = jnp.where(yy == 0, n_all[:, 0:k_half], n_all[:, k_half:])
            inv_col = _col(1.0 / (n_own + EPS_COUNT))
            for cp in s_copies:
                cp.wait_recv()
            sq_acc = jnp.zeros((k_half, 128), jnp.float32)
            for g in range(h_dim // 128):
                cols = slice(g * 128, (g + 1) * 128)
                mu = (s_v[pl.ds(mine, k_half), cols] + s_rx[t, :, cols]) * inv_col
                mu_b[pl.ds(mine, k_half), cols] = mu.astype(jnp.bfloat16)
                sq_acc = sq_acc + mu * mu
            mu_copy = pltpu.make_async_remote_copy(
                src_ref=mu_b.at[pl.ds(mine, k_half)], dst_ref=mu_b.at[pl.ds(mine, k_half)],
                send_sem=as_sem.at[t], recv_sem=ar_sem.at[t], device_id=y_peer, device_id_type=MESH,
            )
            mu_copy.start()
            c_own = jnp.log((n_own + PRIOR_ALPHA) / log_denom) - beta_ref[t + 1] * _lane_sum_row(sq_acc)
            c_tx[t] = c_own
            c_copy = pltpu.make_async_remote_copy(
                src_ref=c_tx.at[t], dst_ref=c_rx.at[t], send_sem=cs_sem.at[t], recv_sem=cr_sem.at[t],
                device_id=y_peer, device_id_type=MESH,
            )
            c_copy.start()
            c_copy.wait_recv()
            c_peer_row = c_rx[t]
            c_row = jnp.concatenate(
                [jnp.where(yy == 0, c_own, c_peer_row), jnp.where(yy == 0, c_peer_row, c_own)], axis=1
            )
            c_col = _col(c_row)
            mu_copy.wait_recv()
            mu_copy.wait_send()
            c_copy.wait_send()
        else:
            lse_copy = pltpu.make_async_remote_copy(
                src_ref=lse_v.at[:, pl.ds(own_rows, own_rows)], dst_ref=lse_rx,
                send_sem=ls_sem.at[0], recv_sem=lr_sem.at[0], device_id=c_peer, device_id_type=MESH,
            )
            lse_copy.start()
            n_copy.wait_recv()
            n_all = n_part + n_rx[t]
            lp_row = jnp.log((n_all + PRIOR_ALPHA) / log_denom)
            n_tx[t + 1] = lp_row
            lp_copy = pltpu.make_async_remote_copy(
                src_ref=n_tx.at[t + 1], dst_ref=lp_rx,
                send_sem=ls_sem.at[1], recv_sem=lr_sem.at[1], device_id=c_peer, device_id_type=MESH,
            )
            lp_copy.start()
            inv_col = _col(1.0 / (n_all + EPS_COUNT))
            out_copies = []
            for i in range(4):
                hi = i % 2
                base = mine if i < 2 else theirs
                s_copies[i].wait_recv()
                inv_half = jnp.where(yy == (0 if i < 2 else 1), inv_col[0:k_half, :], inv_col[k_half:, :])
                for g in range(h_dim // 256):
                    cols = slice(hi * (h_dim // 2) + g * 128, hi * (h_dim // 2) + (g + 1) * 128)
                    mu_out[fit, pl.ds(base, k_half), cols] = (
                        s_v[pl.ds(base, k_half), cols] + s_rx_last[pl.ds(base, k_half), cols]
                    ) * inv_half
                half = slice(hi * (h_dim // 2), (hi + 1) * (h_dim // 2))
                cp = pltpu.make_async_remote_copy(
                    src_ref=mu_out.at[fit, pl.ds(base, k_half), half],
                    dst_ref=mu_out.at[fit, pl.ds(base, k_half), half],
                    send_sem=os_sem.at[i], recv_sem=or_sem.at[i], device_id=c_peer, device_id_type=MESH,
                )
                cp.start()
                out_copies.append(cp)
            lse_copy.wait_recv()
            own_lse = lse_v[:, 0:own_rows]
            lse_out[0:1, :] = jnp.where(core == 0, own_lse, lse_rx[...])
            lse_out[1:2, :] = jnp.where(core == 0, lse_rx[...], own_lse)
            lp_copy.wait_recv()
            lp_out[0:1, :] = jnp.where(core == 0, lp_row, lp_rx[...])
            lp_out[1:2, :] = jnp.where(core == 0, lp_rx[...], lp_row)
            lse_copy.wait_send()
            lp_copy.wait_send()
            for cp in out_copies:
                cp.wait_send()
                cp.wait_recv()
        n_copy.wait_send()
        for cp in s_copies:
            cp.wait_send()
        for copies in z_copies:
            for cp in copies:
                cp.wait_send()
    for cp in swaps:
        cp.wait_send()


def solution(mesh):
    n_z = mesh.shape["comp"]
    row_size = mesh.shape["row"]

    def local_fit(x_local, mu_init, logpi_init, inv_temp):
        n_rows, full_dim = x_local.shape
        _, k_dim, h_dim = mu_init.shape
        n_sweeps = inv_temp.shape[0]
        total = 2 * n_rows
        chunk = total // N_CHUNKS
        k_half = k_dim // 2
        log_denom = float(n_rows * row_size + k_dim * n_z * PRIOR_ALPHA)
        f32 = jnp.float32
        bf16 = jnp.bfloat16
        dma = pltpu.SemaphoreType.DMA
        mu, lp, lse = pl.pallas_call(
            functools.partial(em_kernel, n_z, n_sweeps, log_denom),
            out_shape=(
                jax.ShapeDtypeStruct((2, k_dim, h_dim), f32),
                jax.ShapeDtypeStruct((2, k_dim), f32),
                jax.ShapeDtypeStruct((2, n_rows), f32),
            ),
            in_specs=[
                pl.BlockSpec(memory_space=pl.ANY),
                pl.BlockSpec(memory_space=pl.ANY),
                pl.BlockSpec(memory_space=pltpu.VMEM),
                pl.BlockSpec(memory_space=pltpu.SMEM),
            ],
            out_specs=(
                pl.BlockSpec(memory_space=pltpu.VMEM),
                pl.BlockSpec(memory_space=pltpu.VMEM),
                pl.BlockSpec(memory_space=pltpu.VMEM),
            ),
            scratch_shapes=[
                pltpu.VMEM((total, h_dim), bf16),
                pltpu.VMEM((k_dim, h_dim), f32),
                pltpu.VMEM((k_dim, h_dim), bf16),
                pltpu.VMEM((k_dim, total), f32),
                pltpu.VMEM((k_dim, total), bf16),
                pltpu.VMEM((k_dim, h_dim), f32),
                pltpu.VMEM((n_sweeps - 1, k_half, h_dim), f32),
                pltpu.VMEM((k_dim, h_dim), f32),
                pltpu.VMEM((n_sweeps + 1, 1, k_dim), f32),
                pltpu.VMEM((n_sweeps, 1, k_dim), f32),
                pltpu.VMEM((n_sweeps, 1, k_half), f32),
                pltpu.VMEM((n_sweeps, 1, k_half), f32),
                pltpu.VMEM((n_sweeps, N_CHUNKS, 1, chunk), f32),
                pltpu.VMEM((n_sweeps, N_CHUNKS, n_z - 1, 1, chunk), f32),
                pltpu.VMEM((1, total), f32),
                pltpu.VMEM((1, total), f32),
                pltpu.VMEM((1, total), f32),
                pltpu.VMEM((1, n_rows), f32),
                pltpu.VMEM((1, k_dim), f32),
                dma((1 + N_CHUNKS // 2,)),
                dma((N_CHUNKS // 2,)), dma((N_CHUNKS // 2,)),
                dma((n_sweeps, N_CHUNKS, n_z - 1)), dma((n_sweeps, N_CHUNKS, n_z - 1)),
                dma((n_sweeps, 4)), dma((n_sweeps, 4)),
                dma((n_sweeps,)), dma((n_sweeps,)),
                dma((n_sweeps,)), dma((n_sweeps,)),
                dma((n_sweeps,)), dma((n_sweeps,)),
                dma((2,)), dma((2,)),
                dma((4,)), dma((4,)),
            ],
            compiler_params=pltpu.CompilerParams(
                collective_id=0, has_side_effects=True, vmem_limit_bytes=60 * 1024 * 1024
            ),
            name="em_kernel",
        )(x_local, mu_init, logpi_init, inv_temp)
        return mu, lp, lse

    return jax.shard_map(
        local_fit,
        mesh=mesh,
        in_specs=(P(("grp", "row"), None), P(None, ("grp", "comp"), None), P(None, ("grp", "comp")), P()),
        out_specs=(P(None, ("grp", "comp"), None), P(None, ("grp", "comp")), P(None, ("grp", "row"))),
        check_vma=False,
    )
```

time: 285 us -> 68.1 us (0.24)
  blocking collectives: 123 us -> 0 us
  waiting for transfers between devices: 83.9 us -> 0 us
  Pallas kernels: 0 us -> 62.3 us
  matrix products: 33.3 us -> 0 us
  other arithmetic: 28.4 us -> 0 us
  between operations: 13.8 us -> 0.64 us
  local copies, waits for them, and re-layouts: 1.81 us -> 4.82 us
    psum x3 -> x0, waiting for transfers between devices: 83.8 us -> none  [local_fit(): counts, stat_sum = lax.psum((counts, stat_sum), 'row')]
    psum x6 -> x0, blocking collectives: 65 us -> none  [the longest x3 46.7 us: local_fit(): row_sum = lax.psum(jnp.sum(shifted, axis=2), 'comp')]
    pallas_call x0 -> x1, Pallas kernels: none -> 62.3 us  [local_fit(): pl.pallas_call(functools.partial(em_kernel, n_z, n_sweeps, log_denom), ou...]
    pmax x3 -> x0, blocking collectives: 57.9 us -> none  [local_fit(): row_max = lax.pmax(jnp.max(logits, axis=2), 'comp')]
    dot_general x6 -> x0, matrix products: 33.3 us -> none  [the longest x3 17.5 us: local_fit(): jnp.einsum('snh,skh->snk', x_fits, mean_vecs.astype(jnp.bfloat16), prefer...]
    reduce_sum x10 -> x0, other arithmetic: 24.9 us -> none  [the longest x3 9.01 us: local_fit(): counts = jnp.sum(resp_f, axis=1)]
    unnamed x8 -> x3, local copies, waits for them, and re-layouts: 0.36 us -> 4.82 us
  transfers between devices with their start and end apart: 3 -> 0, of which waited for: 3 -> 0; matrix products, arithmetic and copies ran while one was open for 3% -> 0% of each run, Pallas kernels for 0% -> 0%
where the time goes in v1:
time: 68.1 us; the launch traced here: 67.8 us
  Pallas kernels  62.3 us (91%)
  local copies, waits for them, and re-layouts  4.82 us (7%)
    pallas_call x1, Pallas kernels, local_fit(): pl.pallas_call(functools.partial(em_kernel, n_z, n_sweeps, log_denom), ou...  62.3 us
    unnamed x3, local copies, waits for them, and re-layouts  4.82 us

profile of v1, /device:TPU:0, one launch (start us, length us, event | category | flops | bytes accessed | tf_op | source)
XLA Modules:
  0.0 67.8 jit_solution(12103051579957527733)
XLA Ops:
  0.6 62.3 %em_kernel.1 = (f32[2,256,512]{2,1,0:T(8,128)}, f32[2,256]{1,0:T(2,128)}, f32[2,2048]{1,0:T(2,128)}) custom-call(bf16[2048,1024]{1,0:T(8,128)(2,1)} %x_hbm.1, f32[2,256,512]{2,1,0:T(8,128)} %mu_hbm.1, f32[2,256]{1,0:T(2,128)} %lp_ref.1, f32[3]{0:T(128)} %beta_ref.1), custom_call_target="tpu_custom_call" | custom-call | tf_op jit(solution)/shard_map/em_kernel/pallas_call | solution.py:317
  62.9 2.3 %copy.10 = f32[2,256,512]{2,1,0:T(8,128)} copy(f32[2,256,512]{2,1,0:T(8,128)} %get-tuple-element.6) | data formatting | bytes 2097152
  65.2 1.2 %copy.11 = f32[2,256]{1,0:T(2,128)} copy(f32[2,256]{1,0:T(2,128)} %get-tuple-element.7) | data formatting | bytes 4096
  66.4 1.3 %copy.12 = f32[2,2048]{1,0:T(2,128)} copy(f32[2,2048]{1,0:T(2,128)} %get-tuple-element.8) | data formatting | bytes 32768

commit v2 on v1

v2 whole, which is shorter than its diff:
```python
import functools

import jax
import jax.numpy as jnp
from jax import lax
from jax.experimental import pallas as pl
from jax.experimental.pallas import tpu as pltpu
from jax.sharding import PartitionSpec as P

EPS_COUNT = 1e-6
PRIOR_ALPHA = 1e-3
MESH = pl.DeviceIdType.MESH
LANE_BLOCK = 512
N_CHUNKS = 4
VMEM_LIMIT = 40 * 1024 * 1024


def _col(row):
    n = row.shape[1]
    parts = [
        jnp.transpose(jnp.broadcast_to(row[:, i : i + 128], (128, 128)))
        for i in range(0, n, 128)
    ]
    return parts[0] if len(parts) == 1 else jnp.concatenate(parts, axis=0)


def _lane_sum_row(block):
    n = block.shape[0]
    parts = [
        jnp.sum(jnp.transpose(block[i : i + 128, :]), axis=0, keepdims=True)
        for i in range(0, n, 128)
    ]
    return parts[0] if len(parts) == 1 else jnp.concatenate(parts, axis=1)


def _fold(x):
    acc = x[:, 0:128]
    for i in range(128, x.shape[1], 128):
        acc = acc + x[:, i : i + 128]
    return acc


def em_kernel(
    n_z, n_sweeps, log_denom,
    x_hbm, mu_hbm, lp_hbm, beta_hbm,
    mu_out, lp_out, lse_out,
    x_v, mu_f, mu_b, p_v, r_v, s_v, s_rx, s_rx_last, n_tx, n_rx, c_tx, c_rx,
    z_tx, z_rx, m_v, sqx_v, lse_v, lse_rx, lp_rx, lp_v, beta_ref,
    ld_sem, xs_sem, xr_sem, zs_sem, zr_sem, ss_sem, sr_sem, ns_sem, nr_sem,
    as_sem, ar_sem, cs_sem, cr_sem, ls_sem, lr_sem, os_sem, or_sem, turn_sem,
):
    row = lax.axis_index("row")
    zz = lax.axis_index("comp")
    core = lax.rem(row, 2)
    yy = lax.div(row, 2)
    fit = core
    other = 1 - core
    y_peer = {"row": (1 - yy) * 2 + core}
    c_peer = {"row": yy * 2 + (1 - core)}
    z_peers = [{"comp": lax.rem(zz + d, n_z)} for d in range(1, n_z)]

    n_rows = x_v.shape[0]
    own_rows = n_rows // 2
    k_dim, h_dim = mu_f.shape
    k_half = k_dim // 2
    chunk = n_rows // N_CHUNKS
    per_chunk = chunk // LANE_BLOCK
    mine = pl.multiple_of(yy * k_half, k_half)
    theirs = pl.multiple_of((1 - yy) * k_half, k_half)
    own_chunks = N_CHUNKS // 2
    col_blocks = [slice(g * 128, (g + 1) * 128) for g in range(h_dim // 128)]

    barrier = pltpu.get_barrier_semaphore()
    for peer in [c_peer, y_peer] + z_peers:
        pl.semaphore_signal(barrier, inc=1, device_id=peer, device_id_type=MESH)

    beta_load = pltpu.make_async_copy(beta_hbm, beta_ref, ld_sem.at[0])
    lp_load = pltpu.make_async_copy(lp_hbm, lp_v, ld_sem.at[1])
    mu_load = pltpu.make_async_copy(mu_hbm.at[fit], mu_f, ld_sem.at[2])
    for cp in (beta_load, lp_load, mu_load):
        cp.start()
    loads = []
    for i in range(own_chunks):
        cp = pltpu.make_async_copy(
            x_hbm.at[pl.ds(i * chunk, chunk), pl.ds(pl.multiple_of(fit * h_dim, h_dim), h_dim)],
            x_v.at[pl.ds(i * chunk, chunk)],
            ld_sem.at[3 + i],
        )
        cp.start()
        loads.append(cp)

    with jax.named_scope("enter"):
        pl.semaphore_wait(barrier, 1 + n_z)

    swaps = []
    for i in range(own_chunks):
        cp = pltpu.make_async_remote_copy(
            src_ref=x_hbm.at[pl.ds(i * chunk, chunk), pl.ds(pl.multiple_of(other * h_dim, h_dim), h_dim)],
            dst_ref=x_v.at[pl.ds(own_rows + i * chunk, chunk)],
            send_sem=xs_sem.at[i],
            recv_sem=xr_sem.at[i],
            device_id=c_peer,
            device_id_type=MESH,
        )
        cp.start()
        swaps.append(cp)

    with jax.named_scope("init"):
        beta_load.wait()
        lp_load.wait()
        mu_load.wait()
        mu0 = mu_f[...]
        mu_b[...] = mu0.astype(jnp.bfloat16)
        lp0 = jnp.where(core == 0, lp_v[0:1, :], lp_v[1:2, :])
        c_row = lp0 - beta_ref[0] * _lane_sum_row(_fold(mu0 * mu0))
        c_col = _col(c_row)

    mu_copies = []
    for t in range(n_sweeps):
        last = t == n_sweeps - 1
        beta = beta_ref[t]
        z_copies = []
        for ci in range(N_CHUNKS):
            if t == 0:
                with jax.named_scope("xwait"):
                    if ci < own_chunks:
                        loads[ci].wait()
                    else:
                        swaps[ci - own_chunks].wait_recv()
            with jax.named_scope("estep"):
                for bi in range(per_chunk):
                    r0 = ci * chunk + bi * LANE_BLOCK
                    a = lax.dot_general(
                        mu_b[...], x_v[r0 : r0 + LANE_BLOCK, :],
                        (((1,), (1,)), ((), ())), preferred_element_type=jnp.float32,
                    )
                    lg = a * (2.0 * beta) + jnp.concatenate([c_col] * (LANE_BLOCK // 128), axis=1)
                    m = jnp.max(lg, axis=0, keepdims=True)
                    p = jnp.exp(lg - m)
                    l = m + jnp.log(jnp.sum(p, axis=0, keepdims=True))
                    p_v[:, r0 : r0 + LANE_BLOCK] = p
                    m_v[:, r0 : r0 + LANE_BLOCK] = m
                    z_tx[t, ci, :, bi * LANE_BLOCK : (bi + 1) * LANE_BLOCK] = l
            copies = []
            for d, peer in enumerate(z_peers):
                cp = pltpu.make_async_remote_copy(
                    src_ref=z_tx.at[t, ci],
                    dst_ref=z_rx.at[t, ci, d],
                    send_sem=zs_sem.at[t, ci, d],
                    recv_sem=zr_sem.at[t, ci, d],
                    device_id=peer,
                    device_id_type=MESH,
                )
                cp.start()
                copies.append(cp)
            z_copies.append(copies)

        n_acc = jnp.zeros((k_dim, 128), jnp.float32)
        for ci in range(N_CHUNKS):
            with jax.named_scope("zwait"):
                for cp in z_copies[ci]:
                    cp.wait_recv()
            with jax.named_scope("resp"):
                for bi in range(per_chunk):
                    r0 = ci * chunk + bi * LANE_BLOCK
                    sl = slice(bi * LANE_BLOCK, (bi + 1) * LANE_BLOCK)
                    parts = [z_tx[t, ci, :, sl]] + [z_rx[t, ci, d, :, sl] for d in range(n_z - 1)]
                    top = functools.reduce(jnp.maximum, parts)
                    tot = functools.reduce(lambda u, v: u + v, [jnp.exp(q - top) for q in parts])
                    lse = top + jnp.log(tot)
                    scale = jnp.exp(m_v[:, r0 : r0 + LANE_BLOCK] - lse)
                    r = p_v[:, r0 : r0 + LANE_BLOCK] * scale
                    r_v[:, r0 : r0 + LANE_BLOCK] = r.astype(jnp.bfloat16)
                    n_acc = n_acc + _fold(r)
                    if last:
                        lse_v[:, r0 : r0 + LANE_BLOCK] = lse - beta * sqx_v[:, r0 : r0 + LANE_BLOCK]
                rows = slice(ci * chunk, (ci + 1) * chunk)
                part = jnp.dot(
                    r_v[pl.ds(theirs, k_half), rows], x_v[rows, :], preferred_element_type=jnp.float32
                )
                s_v[pl.ds(theirs, k_half), :] = part if ci == 0 else s_v[pl.ds(theirs, k_half), :] + part

        n_part = _lane_sum_row(n_acc)
        n_tx[t] = n_part
        n_copy = pltpu.make_async_remote_copy(
            src_ref=n_tx.at[t], dst_ref=n_rx.at[t], send_sem=ns_sem.at[t], recv_sem=nr_sem.at[t],
            device_id=y_peer, device_id_type=MESH,
        )
        n_copy.start()
        if t == 0:
            with jax.named_scope("turn"):
                @pl.when(core == 0)
                def _():
                    pl.semaphore_wait(turn_sem, 1)
        s_copies = []

        def send_s(half, g, slot):
            dst = s_rx_last.at[pl.ds(half, k_half), col_blocks[g]] if last else s_rx.at[t, :, col_blocks[g]]
            cp = pltpu.make_async_remote_copy(
                src_ref=s_v.at[pl.ds(half, k_half), col_blocks[g]], dst_ref=dst,
                send_sem=ss_sem.at[t, slot], recv_sem=sr_sem.at[t, slot],
                device_id=y_peer, device_id_type=MESH,
            )
            cp.start()
            s_copies.append(cp)

        for g in range(len(col_blocks)):
            send_s(theirs, g, g)
        with jax.named_scope("smine"):
            s_v[pl.ds(mine, k_half), :] = jnp.dot(
                r_v[pl.ds(mine, k_half), :], x_v[...], preferred_element_type=jnp.float32
            )
        if last:
            for g in range(len(col_blocks)):
                send_s(mine, g, len(col_blocks) + g)

        if t == 0:
            with jax.named_scope("pass"):
                for cp in s_copies:
                    cp.wait_send()
                @pl.when(core == 1)
                def _():
                    pl.semaphore_signal(turn_sem, inc=1, device_id=c_peer, device_id_type=MESH)
            with jax.named_scope("sqx"):
                ones = jnp.ones((16, h_dim), jnp.bfloat16)
                for b in range(n_rows // 512):
                    r0 = b * 512
                    xf = x_v[r0 : r0 + 512, :].astype(jnp.float32)
                    sq = xf * xf
                    hi_part = sq.astype(jnp.bfloat16)
                    lo_part = (sq - hi_part.astype(jnp.float32)).astype(jnp.bfloat16)
                    acc = lax.dot_general(ones, hi_part, (((1,), (1,)), ((), ())), preferred_element_type=jnp.float32)
                    acc = acc + lax.dot_general(ones, lo_part, (((1,), (1,)), ((), ())), preferred_element_type=jnp.float32)
                    sqx_v[:, r0 : r0 + 512] = acc[0:1, :]

        if not last:
            with jax.named_scope("nwait"):
                n_copy.wait_recv()
            n_all = n_part + n_rx[t]
            n_own = jnp.where(yy == 0, n_all[:, 0:k_half], n_all[:, k_half:])
            inv_col = _col(1.0 / (n_own + EPS_COUNT))
            sq_acc = jnp.zeros((k_half, 128), jnp.float32)
            mu_copies = []
            for g, cols in enumerate(col_blocks):
                with jax.named_scope("ywait"):
                    s_copies[g].wait_recv()
                with jax.named_scope("mu"):
                    mu = (s_v[pl.ds(mine, k_half), cols] + s_rx[t, :, cols]) * inv_col
                    mu_b[pl.ds(mine, k_half), cols] = mu.astype(jnp.bfloat16)
                    sq_acc = sq_acc + mu * mu
                cp = pltpu.make_async_remote_copy(
                    src_ref=mu_b.at[pl.ds(mine, k_half), cols], dst_ref=mu_b.at[pl.ds(mine, k_half), cols],
                    send_sem=as_sem.at[t, g], recv_sem=ar_sem.at[t, g], device_id=y_peer, device_id_type=MESH,
                )
                cp.start()
                mu_copies.append(cp)
            c_own = jnp.log((n_own + PRIOR_ALPHA) / log_denom) - beta_ref[t + 1] * _lane_sum_row(sq_acc)
            c_tx[t] = c_own
            c_copy = pltpu.make_async_remote_copy(
                src_ref=c_tx.at[t], dst_ref=c_rx.at[t], send_sem=cs_sem.at[t], recv_sem=cr_sem.at[t],
                device_id=y_peer, device_id_type=MESH,
            )
            c_copy.start()
            with jax.named_scope("cwait"):
                c_copy.wait_recv()
            c_peer_row = c_rx[t]
            c_row = jnp.concatenate(
                [jnp.where(yy == 0, c_own, c_peer_row), jnp.where(yy == 0, c_peer_row, c_own)], axis=1
            )
            c_col = _col(c_row)
            with jax.named_scope("muwait"):
                for cp in mu_copies:
                    cp.wait_recv()
                for cp in mu_copies:
                    cp.wait_send()
                c_copy.wait_send()
        else:
            lse_copy = pltpu.make_async_remote_copy(
                src_ref=lse_v.at[:, pl.ds(own_rows, own_rows)], dst_ref=lse_rx,
                send_sem=ls_sem.at[0], recv_sem=lr_sem.at[0], device_id=c_peer, device_id_type=MESH,
            )
            lse_copy.start()
            n_copy.wait_recv()
            n_all = n_part + n_rx[t]
            lp_row = jnp.log((n_all + PRIOR_ALPHA) / log_denom)
            n_tx[t + 1] = lp_row
            lp_copy = pltpu.make_async_remote_copy(
                src_ref=n_tx.at[t + 1], dst_ref=lp_rx,
                send_sem=ls_sem.at[1], recv_sem=lr_sem.at[1], device_id=c_peer, device_id_type=MESH,
            )
            lp_copy.start()
            inv_col = _col(1.0 / (n_all + EPS_COUNT))
            lse_copy.wait_recv()
            own_lse = lse_v[:, 0:own_rows]
            lse_out[0:1, :] = jnp.where(core == 0, own_lse, lse_rx[...])
            lse_out[1:2, :] = jnp.where(core == 0, lse_rx[...], own_lse)
            lp_copy.wait_recv()
            lp_out[0:1, :] = jnp.where(core == 0, lp_row, lp_rx[...])
            lp_out[1:2, :] = jnp.where(core == 0, lp_rx[...], lp_row)
            out_copies = []
            for half in range(2):
                base = mine if half == 0 else theirs
                inv_half = jnp.where(yy == half, inv_col[0:k_half, :], inv_col[k_half:, :])
                for g, cols in enumerate(col_blocks):
                    slot = half * len(col_blocks) + g
                    with jax.named_scope("fwait"):
                        s_copies[slot].wait_recv()
                    with jax.named_scope("fmu"):
                        mu_out[fit, pl.ds(base, k_half), cols] = (
                            s_v[pl.ds(base, k_half), cols] + s_rx_last[pl.ds(base, k_half), cols]
                        ) * inv_half
                    cp = pltpu.make_async_remote_copy(
                        src_ref=mu_out.at[fit, pl.ds(base, k_half), cols],
                        dst_ref=mu_out.at[fit, pl.ds(base, k_half), cols],
                        send_sem=os_sem.at[slot], recv_sem=or_sem.at[slot], device_id=c_peer, device_id_type=MESH,
                    )
                    cp.start()
                    out_copies.append(cp)
            lse_copy.wait_send()
            lp_copy.wait_send()
            with jax.named_scope("owait"):
                for cp in out_copies:
                    cp.wait_send()
                    cp.wait_recv()
        with jax.named_scope("tail"):
            n_copy.wait_send()
            if t > 0:
                for cp in s_copies:
                    cp.wait_send()
            for copies in z_copies:
                for cp in copies:
                    cp.wait_send()
    for cp in swaps:
        cp.wait_send()


def store_kernel(mu_ref, lp_ref, lse_ref, mu_out, lp_out, lse_out, sems):
    copies = []
    parts = 4
    step = mu_ref.shape[1] // parts
    for s in range(mu_ref.shape[0]):
        for i in range(parts):
            rows = pl.ds(i * step, step)
            copies.append(
                pltpu.make_async_copy(mu_ref.at[s, rows], mu_out.at[s, rows], sems.at[2 + s * parts + i])
            )
    copies.append(pltpu.make_async_copy(lp_ref, lp_out, sems.at[0]))
    copies.append(pltpu.make_async_copy(lse_ref, lse_out, sems.at[1]))
    for cp in copies:
        cp.start()
    for cp in copies:
        cp.wait()


def solution(mesh):
    n_z = mesh.shape["comp"]
    row_size = mesh.shape["row"]

    def local_fit(x_local, mu_init, logpi_init, inv_temp):
        n_rows, full_dim = x_local.shape
        _, k_dim, h_dim = mu_init.shape
        n_sweeps = inv_temp.shape[0]
        total = 2 * n_rows
        chunk = total // N_CHUNKS
        k_half = k_dim // 2
        col_blocks = h_dim // 128
        log_denom = float(n_rows * row_size + k_dim * n_z * PRIOR_ALPHA)
        f32 = jnp.float32
        bf16 = jnp.bfloat16
        dma = pltpu.SemaphoreType.DMA
        mu, lp, lse = pl.pallas_call(
            functools.partial(em_kernel, n_z, n_sweeps, log_denom),
            out_shape=(
                pltpu.VMEM((2, k_dim, h_dim), f32),
                pltpu.VMEM((2, k_dim), f32),
                pltpu.VMEM((2, n_rows), f32),
            ),
            in_specs=[pl.BlockSpec(memory_space=pltpu.HBM)] * 4,
            out_specs=(
                pl.BlockSpec(memory_space=pltpu.VMEM),
                pl.BlockSpec(memory_space=pltpu.VMEM),
                pl.BlockSpec(memory_space=pltpu.VMEM),
            ),
            scratch_shapes=[
                pltpu.VMEM((total, h_dim), bf16),
                pltpu.VMEM((k_dim, h_dim), f32),
                pltpu.VMEM((k_dim, h_dim), bf16),
                pltpu.VMEM((k_dim, total), f32),
                pltpu.VMEM((k_dim, total), bf16),
                pltpu.VMEM((k_dim, h_dim), f32),
                pltpu.VMEM((n_sweeps - 1, k_half, h_dim), f32),
                pltpu.VMEM((k_dim, h_dim), f32),
                pltpu.VMEM((n_sweeps + 1, 1, k_dim), f32),
                pltpu.VMEM((n_sweeps, 1, k_dim), f32),
                pltpu.VMEM((n_sweeps, 1, k_half), f32),
                pltpu.VMEM((n_sweeps, 1, k_half), f32),
                pltpu.VMEM((n_sweeps, N_CHUNKS, 1, chunk), f32),
                pltpu.VMEM((n_sweeps, N_CHUNKS, n_z - 1, 1, chunk), f32),
                pltpu.VMEM((1, total), f32),
                pltpu.VMEM((1, total), f32),
                pltpu.VMEM((1, total), f32),
                pltpu.VMEM((1, n_rows), f32),
                pltpu.VMEM((1, k_dim), f32),
                pltpu.VMEM((2, k_dim), f32),
                pltpu.SMEM((n_sweeps,), f32),
                dma((3 + N_CHUNKS // 2,)),
                dma((N_CHUNKS // 2,)), dma((N_CHUNKS // 2,)),
                dma((n_sweeps, N_CHUNKS, n_z - 1)), dma((n_sweeps, N_CHUNKS, n_z - 1)),
                dma((n_sweeps, 2 * col_blocks)), dma((n_sweeps, 2 * col_blocks)),
                dma((n_sweeps,)), dma((n_sweeps,)),
                dma((n_sweeps, col_blocks)), dma((n_sweeps, col_blocks)),
                dma((n_sweeps,)), dma((n_sweeps,)),
                dma((2,)), dma((2,)),
                dma((2 * col_blocks,)), dma((2 * col_blocks,)),
                pltpu.SemaphoreType.REGULAR,
            ],
            compiler_params=pltpu.CompilerParams(
                collective_id=0, has_side_effects=True, vmem_limit_bytes=VMEM_LIMIT
            ),
            name="em_kernel",
        )(*[pltpu.with_memory_space_constraint(v, pltpu.HBM) for v in (x_local, mu_init, logpi_init, inv_temp)])
        return pl.pallas_call(
            store_kernel,
            out_shape=(
                jax.ShapeDtypeStruct((2, k_dim, h_dim), f32),
                jax.ShapeDtypeStruct((2, k_dim), f32),
                jax.ShapeDtypeStruct((2, n_rows), f32),
            ),
            in_specs=[pl.BlockSpec(memory_space=pltpu.VMEM)] * 3,
            out_specs=(pl.BlockSpec(memory_space=pl.ANY),) * 3,
            scratch_shapes=[dma((2 + 2 * 4,))],
            compiler_params=pltpu.CompilerParams(vmem_limit_bytes=4 * 1024 * 1024),
            name="store_kernel",
        )(mu, lp, lse)

    return jax.shard_map(
        local_fit,
        mesh=mesh,
        in_specs=(P(("grp", "row"), None), P(None, ("grp", "comp"), None), P(None, ("grp", "comp")), P()),
        out_specs=(P(None, ("grp", "comp"), None), P(None, ("grp", "comp")), P(None, ("grp", "row"))),
        check_vma=False,
    )
```

time: 68.1 us -> 61.6 us (0.905)
  local copies, waits for them, and re-layouts: 4.82 us -> 0 us
  Pallas kernels: 62.3 us -> 60.6 us
    unnamed x3 -> x0, local copies, waits for them, and re-layouts: 4.82 us -> none
    pallas_call x1, Pallas kernels: 62.3 us -> 59.6 us  [local_fit(): pl.pallas_call(functools.partial(em_kernel, n_z, n_sweeps, log_denom), ou...]
    pallas_call x0 -> x1, Pallas kernels: none -> 1.05 us  [local_fit(): pl.pallas_call(store_kernel, out_shape=(jax.ShapeDtypeStruct((2, k_dim, h...]
where the time goes in v2:
time: 61.6 us; the launch traced here: 61.4 us
  Pallas kernels  60.6 us (98%)
  between operations  0.8 us (1%)
    pallas_call x1, Pallas kernels, local_fit(): pl.pallas_call(functools.partial(em_kernel, n_z, n_sweeps, log_denom), ou...  59.6 us

profile of v2, /device:TPU:0, one launch (start us, length us, event | category | flops | bytes accessed | tf_op | source)
XLA Modules:
  0.0 61.4 jit_solution(2744781835151672410)
XLA Ops:
  0.6 59.6 %em_kernel.1 = (f32[2,256,512]{2,1,0:T(8,128)S(1)}, f32[2,256]{1,0:T(2,128)S(1)}, f32[2,2048]{1,0:T(2,128)S(1)}) custom-call(bf16[2048,1024]{1,0:T(8,128)(2,1)} %x_hbm.1, f32[2,256,512]{2,1,0:T(8,128)} %mu_hbm.1, f32[2,256]{1,0:T(2,128)} %lp_hbm.1, f32[3]{0:T(128)} %beta_hbm.1), custom_call_target="tpu_custom_call" | custom-call | tf_op jit(solution)/shard_map/em_kernel/pallas_call | solution.py:371
  60.2 1.1 %store_kernel.1 = (f32[2,256,512]{2,1,0:T(8,128)}, f32[2,256]{1,0:T(2,128)}, f32[2,2048]{1,0:T(2,128)}) custom-call(f32[2,256,512]{2,1,0:T(8,128)S(1)} %get-tuple-element.6.mu_ref, f32[2,256]{1,0:T(2,128)S(1)} %get-tuple-element.7.lp_ref, f32[2,2048]{1,0:T(2,128)S(1)} %get-tuple-element.8.lse_ref), custom_call_target="tpu_custom_call" | custom-call | tf_op jit(solution)/shard_map/store_kernel/pallas_call | solution.py:422

commit v3 on v2

v3 whole, which is shorter than its diff:
```python
import functools

import jax
import jax.numpy as jnp
from jax import lax
from jax.experimental import pallas as pl
from jax.experimental.pallas import tpu as pltpu
from jax.sharding import PartitionSpec as P

EPS_COUNT = 1e-6
PRIOR_ALPHA = 1e-3
MESH = pl.DeviceIdType.MESH
LANE_BLOCK = 512
N_CHUNKS = 4
VMEM_LIMIT = 40 * 1024 * 1024


def _col(row):
    n = row.shape[1]
    parts = [
        jnp.transpose(jnp.broadcast_to(row[:, i : i + 128], (128, 128)))
        for i in range(0, n, 128)
    ]
    return parts[0] if len(parts) == 1 else jnp.concatenate(parts, axis=0)


def _lane_sum_row(block):
    n = block.shape[0]
    parts = [
        jnp.sum(jnp.transpose(block[i : i + 128, :]), axis=0, keepdims=True)
        for i in range(0, n, 128)
    ]
    return parts[0] if len(parts) == 1 else jnp.concatenate(parts, axis=1)


def _fold(x):
    acc = x[:, 0:128]
    for i in range(128, x.shape[1], 128):
        acc = acc + x[:, i : i + 128]
    return acc


def em_kernel(
    n_z, n_sweeps, log_denom,
    x_hbm, mu_hbm, lp_hbm, beta_hbm,
    mu_out, lp_out, lse_out,
    x_v, x_t, mu_f, mu_b, p_v, r_v, s_v, s_rx, n_tx, n_rx, c_tx, c_rx,
    z_tx, z_rx, m_v, l_v, sqx_v, lse_v, lse_rx, lp_rx, lp_v, beta_ref,
    ld_sem, xs_sem, xr_sem, zs_sem, zr_sem, ss_sem, sr_sem, ns_sem, nr_sem,
    as_sem, ar_sem, cs_sem, cr_sem, ls_sem, lr_sem, os_sem, or_sem, turn_sem,
):
    row = lax.axis_index("row")
    zz = lax.axis_index("comp")
    core = lax.rem(row, 2)
    yy = lax.div(row, 2)
    fit = core
    other = 1 - core
    y_peer = {"row": (1 - yy) * 2 + core}
    c_peer = {"row": yy * 2 + (1 - core)}
    z_peers = [{"comp": lax.rem(zz + d, n_z)} for d in range(1, n_z)]

    n_rows = x_v.shape[0]
    own_rows = n_rows // 2
    k_dim, h_dim = mu_f.shape
    k_half = k_dim // 2
    chunk = n_rows // N_CHUNKS
    per_chunk = chunk // LANE_BLOCK
    mine = pl.multiple_of(yy * k_half, k_half)
    theirs = pl.multiple_of((1 - yy) * k_half, k_half)
    own_chunks = N_CHUNKS // 2
    n_col = h_dim // 128
    col_blocks = [slice(g * 128, (g + 1) * 128) for g in range(n_col)]
    lanes = LANE_BLOCK // 128

    def remote(src, dst, send, recv, peer):
        return pltpu.make_async_remote_copy(
            src_ref=src, dst_ref=dst, send_sem=send, recv_sem=recv, device_id=peer, device_id_type=MESH
        )

    barrier = pltpu.get_barrier_semaphore()
    for peer in [c_peer, y_peer] + z_peers:
        pl.semaphore_signal(barrier, inc=1, device_id=peer, device_id_type=MESH)

    my_cols = pl.ds(pl.multiple_of(fit * h_dim, h_dim), h_dim)
    your_cols = pl.ds(pl.multiple_of(other * h_dim, h_dim), h_dim)
    beta_load = pltpu.make_async_copy(beta_hbm, beta_ref, ld_sem.at[0])
    lp_load = pltpu.make_async_copy(lp_hbm, lp_v, ld_sem.at[1])
    mu_load = pltpu.make_async_copy(mu_hbm.at[fit], mu_f, ld_sem.at[2])
    for cp in (beta_load, lp_load, mu_load):
        cp.start()
    loads = []
    for i in range(own_chunks):
        rows = pl.ds(i * chunk, chunk)
        cp = pltpu.make_async_copy(x_hbm.at[rows, my_cols], x_v.at[rows], ld_sem.at[3 + i])
        cp.start()
        loads.append(cp)

    with jax.named_scope("enter"):
        pl.semaphore_wait(barrier, 1 + n_z)

    swaps = []
    for i in range(own_chunks):
        cp = remote(
            x_hbm.at[pl.ds(i * chunk, chunk), your_cols], x_v.at[pl.ds(own_rows + i * chunk, chunk)],
            xs_sem.at[0], xr_sem.at[i], c_peer,
        )
        cp.start()
        swaps.append(cp)

    with jax.named_scope("init"):
        beta_load.wait()
        lp_load.wait()
        mu_load.wait()
        mu0 = mu_f[...]
        mu_b[...] = mu0.astype(jnp.bfloat16)
        lp0 = jnp.where(core == 0, lp_v[0:1, :], lp_v[1:2, :])
        c_row = lp0 - beta_ref[0] * _lane_sum_row(_fold(mu0 * mu0))
        c_col = _col(c_row)

    def softmax_half(lg, half, base, cols):
        m = jnp.max(lg, axis=0, keepdims=True)
        p = jnp.exp(lg - m)
        p_v[pl.ds(base, k_half), cols] = p
        m_v[half, :, cols] = m
        return m + jnp.log(jnp.sum(p, axis=0, keepdims=True))

    def log_add(u, v):
        top = jnp.maximum(u, v)
        return top + jnp.log(jnp.exp(u - top) + jnp.exp(v - top))

    def half_logits(base, cc, beta, cols):
        a = jnp.dot(mu_b[pl.ds(base, k_half), :], x_t[:, cols], preferred_element_type=jnp.float32)
        return a * (2.0 * beta) + jnp.concatenate([cc] * lanes, axis=1)

    for t in range(n_sweeps):
        last = t == n_sweeps - 1
        beta = beta_ref[t]
        par = t % 2
        for ci in range(N_CHUNKS):
            if t == 0:
                with jax.named_scope("xwait"):
                    if ci < own_chunks:
                        loads[ci].wait()
                    else:
                        swaps[ci - own_chunks].wait_recv()
            with jax.named_scope("estep"):
                for bi in range(per_chunk):
                    r0 = ci * chunk + bi * LANE_BLOCK
                    cols = slice(r0, r0 + LANE_BLOCK)
                    if t == 0:
                        a = lax.dot_general(
                            mu_b[...], x_v[cols, :], (((1,), (1,)), ((), ())), preferred_element_type=jnp.float32
                        )
                        lg = a * (2.0 * beta) + jnp.concatenate([c_col] * lanes, axis=1)
                        l0 = softmax_half(lg[0:k_half, :], 0, 0, cols)
                        l1 = softmax_half(lg[k_half:, :], 1, k_half, cols)
                    else:
                        l0 = l_v[:, cols]
                        l1 = softmax_half(half_logits(theirs, c_their_col, beta, cols), 1 - yy, theirs, cols)
                    z_tx[par, ci, :, bi * LANE_BLOCK : (bi + 1) * LANE_BLOCK] = log_add(l0, l1)
            for d, peer in enumerate(z_peers):
                remote(z_tx.at[par, ci], z_rx.at[par, ci, d], zs_sem.at[par], zr_sem.at[par, ci], peer).start()

        n_acc = jnp.zeros((k_dim, 128), jnp.float32)
        for ci in range(N_CHUNKS):
            with jax.named_scope("zwait"):
                remote(z_rx.at[par, ci], z_rx.at[par, ci], zs_sem.at[par], zr_sem.at[par, ci], z_peers[0]).wait_recv()
            with jax.named_scope("resp"):
                for bi in range(per_chunk):
                    r0 = ci * chunk + bi * LANE_BLOCK
                    cols = slice(r0, r0 + LANE_BLOCK)
                    sl = slice(bi * LANE_BLOCK, (bi + 1) * LANE_BLOCK)
                    parts = [z_tx[par, ci, :, sl]] + [z_rx[par, ci, d, :, sl] for d in range(n_z - 1)]
                    top = functools.reduce(jnp.maximum, parts)
                    tot = functools.reduce(lambda u, v: u + v, [jnp.exp(q - top) for q in parts])
                    lse = top + jnp.log(tot)
                    halves = []
                    for h in range(2):
                        ks = slice(h * k_half, (h + 1) * k_half)
                        r = p_v[ks, cols] * jnp.exp(m_v[h, :, cols] - lse)
                        r_v[ks, cols] = r.astype(jnp.bfloat16)
                        halves.append(_fold(r))
                    n_acc = n_acc + jnp.concatenate(halves, axis=0)
                    if last:
                        lse_v[:, cols] = lse - beta * sqx_v[:, cols]
                rows = slice(ci * chunk, (ci + 1) * chunk)
                part = jnp.dot(r_v[pl.ds(theirs, k_half), rows], x_v[rows, :], preferred_element_type=jnp.float32)
                s_v[pl.ds(theirs, k_half), :] = part if ci == 0 else s_v[pl.ds(theirs, k_half), :] + part

        n_part = _lane_sum_row(n_acc)
        n_tx[par] = n_part
        n_copy = remote(n_tx.at[par], n_rx.at[par], ns_sem.at[0], nr_sem.at[0], y_peer)
        n_copy.start()

        def s_copy(half, g, slot):
            return remote(
                s_v.at[pl.ds(half, k_half), col_blocks[g]], s_rx.at[pl.ds(half, k_half), col_blocks[g]],
                ss_sem.at[0 if g < n_col - 1 else 1], sr_sem.at[slot], y_peer,
            )

        first_copies = [s_copy(theirs, g, g) for g in range(n_col)]
        s_mine = jax.named_scope("smine")
        early = s_v.at[pl.ds(theirs, k_half), pl.ds(0, h_dim - 128)]
        late = s_v.at[pl.ds(theirs, k_half), pl.ds(h_dim - 128, 128)]
        early_sent = remote(early, early, ss_sem.at[0], sr_sem.at[0], y_peer)
        late_sent = remote(late, late, ss_sem.at[1], sr_sem.at[0], y_peer)

        if t > 0:
            for cp in first_copies:
                cp.start()
        else:
            @pl.when(core == 1)
            def _():
                for cp in first_copies:
                    cp.start()

        with s_mine:
            s_v[pl.ds(mine, k_half), :] = jnp.dot(
                r_v[pl.ds(mine, k_half), :], x_v[...], preferred_element_type=jnp.float32
            )
        last_copies = []
        if last:
            last_copies = [s_copy(mine, g, n_col + g) for g in range(n_col)]
            for cp in last_copies:
                cp.start()

        if t == 0:
            with jax.named_scope("xt"):
                for b in range(n_rows // LANE_BLOCK):
                    rows = slice(b * LANE_BLOCK, (b + 1) * LANE_BLOCK)
                    x_t[:, rows] = jnp.transpose(x_v[rows, :])
            with jax.named_scope("turn"):
                @pl.when(core == 1)
                def _():
                    early_sent.wait_send()
                    pl.semaphore_signal(turn_sem, inc=1, device_id=c_peer, device_id_type=MESH)

                @pl.when(core == 0)
                def _():
                    pl.semaphore_wait(turn_sem, 1)
                    for cp in first_copies:
                        cp.start()
                    early_sent.wait_send()

            with jax.named_scope("sqx"):
                for b in range(n_rows // LANE_BLOCK):
                    cols = slice(b * LANE_BLOCK, (b + 1) * LANE_BLOCK)
                    xf = x_t[:, cols].astype(jnp.float32)
                    sqx_v[:, cols] = jnp.sum(xf * xf, axis=0, keepdims=True)

        with jax.named_scope("nwait"):
            n_copy.wait_recv()
        n_all = n_part + n_rx[par]
        if not last:
            n_own = jnp.where(yy == 0, n_all[:, 0:k_half], n_all[:, k_half:])
            inv_col = _col(1.0 / (n_own + EPS_COUNT))
            sq_acc = jnp.zeros((k_half, 128), jnp.float32)
            for g, cols in enumerate(col_blocks):
                with jax.named_scope("ywait"):
                    first_copies[g].wait_recv()
                with jax.named_scope("mu"):
                    mu = (s_v[pl.ds(mine, k_half), cols] + s_rx[pl.ds(mine, k_half), cols]) * inv_col
                    mu_b[pl.ds(mine, k_half), cols] = mu.astype(jnp.bfloat16)
                    sq_acc = sq_acc + mu * mu
                block = mu_b.at[pl.ds(mine, k_half), cols]
                remote(block, block, as_sem.at[0], ar_sem.at[0], y_peer).start()
            c_own = jnp.log((n_own + PRIOR_ALPHA) / log_denom) - beta_ref[t + 1] * _lane_sum_row(sq_acc)
            c_tx[par] = c_own
            c_copy = remote(c_tx.at[par], c_rx.at[par], cs_sem.at[0], cr_sem.at[0], y_peer)
            c_copy.start()
            c_own_col = _col(c_own)
            with jax.named_scope("emine"):
                for b in range(n_rows // LANE_BLOCK):
                    cols = slice(b * LANE_BLOCK, (b + 1) * LANE_BLOCK)
                    l_v[:, cols] = softmax_half(
                        half_logits(mine, c_own_col, beta_ref[t + 1], cols), yy, mine, cols
                    )
            with jax.named_scope("cwait"):
                c_copy.wait_recv()
                c_their_col = _col(c_rx[par])
            with jax.named_scope("muwait"):
                sent, came = mu_b.at[pl.ds(mine, k_half)], mu_b.at[pl.ds(theirs, k_half)]
                remote(sent, came, as_sem.at[0], ar_sem.at[0], y_peer).wait()
                c_copy.wait_send()
        else:
            lse_copy = remote(lse_v.at[:, pl.ds(own_rows, own_rows)], lse_rx, ls_sem.at[0], lr_sem.at[0], c_peer)
            lse_copy.start()
            lp_row = jnp.log((n_all + PRIOR_ALPHA) / log_denom)
            n_tx[1 - par] = lp_row
            lp_copy = remote(n_tx.at[1 - par], lp_rx, ls_sem.at[1], lr_sem.at[1], c_peer)
            lp_copy.start()
            inv_col = _col(1.0 / (n_all + EPS_COUNT))
            lse_copy.wait_recv()
            own_lse = lse_v[:, 0:own_rows]
            lse_out[0:1, :] = jnp.where(core == 0, own_lse, lse_rx[...])
            lse_out[1:2, :] = jnp.where(core == 0, lse_rx[...], own_lse)
            lp_copy.wait_recv()
            lp_out[0:1, :] = jnp.where(core == 0, lp_row, lp_rx[...])
            lp_out[1:2, :] = jnp.where(core == 0, lp_rx[...], lp_row)
            for half in range(2):
                base = mine if half == 0 else theirs
                inv_half = jnp.where(yy == half, inv_col[0:k_half, :], inv_col[k_half:, :])
                for g, cols in enumerate(col_blocks):
                    with jax.named_scope("fwait"):
                        (first_copies if half == 0 else last_copies)[g].wait_recv()
                    with jax.named_scope("fmu"):
                        mu_out[fit, pl.ds(base, k_half), cols] = (
                            s_v[pl.ds(base, k_half), cols] + s_rx[pl.ds(base, k_half), cols]
                        ) * inv_half
                    block = mu_out.at[fit, pl.ds(base, k_half), cols]
                    remote(block, block, os_sem.at[0], or_sem.at[0], c_peer).start()
            lse_copy.wait_send()
            lp_copy.wait_send()
            with jax.named_scope("owait"):
                remote(mu_out.at[fit], mu_out.at[fit], os_sem.at[0], or_sem.at[0], c_peer).wait()
        with jax.named_scope("tail"):
            n_copy.wait_send()
            if last:
                both = s_v.at[:, pl.ds(0, h_dim - 128)]
                remote(both, both, ss_sem.at[0], sr_sem.at[0], y_peer).wait_send()
                both = s_v.at[:, pl.ds(h_dim - 128, 128)]
                remote(both, both, ss_sem.at[1], sr_sem.at[0], y_peer).wait_send()
            else:
                if t > 0:
                    early_sent.wait_send()
                late_sent.wait_send()
            remote(z_rx.at[par], z_rx.at[par], zs_sem.at[par], zr_sem.at[par, 0], z_peers[0]).wait_send()
    sent = x_v.at[pl.ds(own_rows, own_rows)]
    remote(sent, sent, xs_sem.at[0], xr_sem.at[0], c_peer).wait_send()


def store_kernel(mu_ref, lp_ref, lse_ref, mu_out, lp_out, lse_out, sems):
    copies = []
    parts = 4
    step = mu_ref.shape[1] // parts
    for s in range(mu_ref.shape[0]):
        for i in range(parts):
            rows = pl.ds(i * step, step)
            copies.append(
                pltpu.make_async_copy(mu_ref.at[s, rows], mu_out.at[s, rows], sems.at[2 + s * parts + i])
            )
    copies.append(pltpu.make_async_copy(lp_ref, lp_out, sems.at[0]))
    copies.append(pltpu.make_async_copy(lse_ref, lse_out, sems.at[1]))
    for cp in copies:
        cp.start()
    for cp in copies:
        cp.wait()


def solution(mesh):
    n_z = mesh.shape["comp"]
    row_size = mesh.shape["row"]

    def local_fit(x_local, mu_init, logpi_init, inv_temp):
        n_rows, full_dim = x_local.shape
        _, k_dim, h_dim = mu_init.shape
        n_sweeps = inv_temp.shape[0]
        total = 2 * n_rows
        chunk = total // N_CHUNKS
        k_half = k_dim // 2
        col_blocks = h_dim // 128
        log_denom = float(n_rows * row_size + k_dim * n_z * PRIOR_ALPHA)
        f32 = jnp.float32
        bf16 = jnp.bfloat16
        dma = pltpu.SemaphoreType.DMA
        mu, lp, lse = pl.pallas_call(
            functools.partial(em_kernel, n_z, n_sweeps, log_denom),
            out_shape=(
                pltpu.VMEM((2, k_dim, h_dim), f32),
                pltpu.VMEM((2, k_dim), f32),
                pltpu.VMEM((2, n_rows), f32),
            ),
            in_specs=[pl.BlockSpec(memory_space=pltpu.HBM)] * 4,
            out_specs=(
                pl.BlockSpec(memory_space=pltpu.VMEM),
                pl.BlockSpec(memory_space=pltpu.VMEM),
                pl.BlockSpec(memory_space=pltpu.VMEM),
            ),
            scratch_shapes=[
                pltpu.VMEM((total, h_dim), bf16),
                pltpu.VMEM((h_dim, total), bf16),
                pltpu.VMEM((k_dim, h_dim), f32),
                pltpu.VMEM((k_dim, h_dim), bf16),
                pltpu.VMEM((k_dim, total), f32),
                pltpu.VMEM((k_dim, total), bf16),
                pltpu.VMEM((k_dim, h_dim), f32),
                pltpu.VMEM((k_dim, h_dim), f32),
                pltpu.VMEM((2, 1, k_dim), f32),
                pltpu.VMEM((2, 1, k_dim), f32),
                pltpu.VMEM((2, 1, k_half), f32),
                pltpu.VMEM((2, 1, k_half), f32),
                pltpu.VMEM((2, N_CHUNKS, 1, chunk), f32),
                pltpu.VMEM((2, N_CHUNKS, n_z - 1, 1, chunk), f32),
                pltpu.VMEM((2, 1, total), f32),
                pltpu.VMEM((1, total), f32),
                pltpu.VMEM((1, total), f32),
                pltpu.VMEM((1, total), f32),
                pltpu.VMEM((1, n_rows), f32),
                pltpu.VMEM((1, k_dim), f32),
                pltpu.VMEM((2, k_dim), f32),
                pltpu.SMEM((n_sweeps,), f32),
                dma((3 + N_CHUNKS // 2,)),
                dma((1,)), dma((N_CHUNKS // 2,)),
                dma((2,)), dma((2, N_CHUNKS)),
                dma((2,)), dma((2 * col_blocks,)),
                dma((1,)), dma((1,)),
                dma((1,)), dma((1,)),
                dma((1,)), dma((1,)),
                dma((2,)), dma((2,)),
                dma((1,)), dma((1,)),
                pltpu.SemaphoreType.REGULAR,
            ],
            compiler_params=pltpu.CompilerParams(
                collective_id=0, has_side_effects=True, vmem_limit_bytes=VMEM_LIMIT
            ),
            name="em_kernel",
        )(*[pltpu.with_memory_space_constraint(v, pltpu.HBM) for v in (x_local, mu_init, logpi_init, inv_temp)])
        return pl.pallas_call(
            store_kernel,
            out_shape=(
                jax.ShapeDtypeStruct((2, k_dim, h_dim), f32),
                jax.ShapeDtypeStruct((2, k_dim), f32),
                jax.ShapeDtypeStruct((2, n_rows), f32),
            ),
            in_specs=[pl.BlockSpec(memory_space=pltpu.VMEM)] * 3,
            out_specs=(pl.BlockSpec(memory_space=pl.ANY),) * 3,
            scratch_shapes=[dma((2 + 2 * 4,))],
            compiler_params=pltpu.CompilerParams(vmem_limit_bytes=4 * 1024 * 1024),
            name="store_kernel",
        )(mu, lp, lse)

    return jax.shard_map(
        local_fit,
        mesh=mesh,
        in_specs=(P(("grp", "row"), None), P(None, ("grp", "comp"), None), P(None, ("grp", "comp")), P()),
        out_specs=(P(None, ("grp", "comp"), None), P(None, ("grp", "comp")), P(None, ("grp", "row"))),
        check_vma=False,
    )
```

time: 61.6 us -> 56 us (0.909)
  Pallas kernels: 60.6 us -> 55.1 us
    pallas_call x1, Pallas kernels: 59.6 us -> 54 us  [local_fit(): pl.pallas_call(functools.partial(em_kernel, n_z, n_sweeps, log_denom), ou...]
where the time goes in v3:
time: 56 us; the launch traced here: 55.9 us
  Pallas kernels  55.1 us (98%)
  between operations  0.8 us (1%)
    pallas_call x1, Pallas kernels, local_fit(): pl.pallas_call(functools.partial(em_kernel, n_z, n_sweeps, log_denom), ou...  54 us

profile of v3, /device:TPU:0, one launch (start us, length us, event | category | flops | bytes accessed | tf_op | source)
XLA Modules:
  0.0 55.9 jit_solution(3515741617498566155)
XLA Ops:
  0.6 54.0 %em_kernel.1 = (f32[2,256,512]{2,1,0:T(8,128)S(1)}, f32[2,256]{1,0:T(2,128)S(1)}, f32[2,2048]{1,0:T(2,128)S(1)}) custom-call(bf16[2048,1024]{1,0:T(8,128)(2,1)} %x_hbm.1, f32[2,256,512]{2,1,0:T(8,128)} %mu_hbm.1, f32[2,256]{1,0:T(2,128)} %lp_hbm.1, f32[3]{0:T(128)} %beta_hbm.1), custom_call_target="tpu_custom_call" | custom-call | tf_op jit(solution)/shard_map/em_kernel/pallas_call | solution.py:366
  54.7 1.1 %store_kernel.1 = (f32[2,256,512]{2,1,0:T(8,128)}, f32[2,256]{1,0:T(2,128)}, f32[2,2048]{1,0:T(2,128)}) custom-call(f32[2,256,512]{2,1,0:T(8,128)S(1)} %get-tuple-element.6.mu_ref, f32[2,256]{1,0:T(2,128)S(1)} %get-tuple-element.7.lp_ref, f32[2,2048]{1,0:T(2,128)S(1)} %get-tuple-element.8.lse_ref), custom_call_target="tpu_custom_call" | custom-call | tf_op jit(solution)/shard_map/store_kernel/pallas_call | solution.py:418

commit v4 on v3

--- a/solution.py
+++ b/solution.py
@@ -11,7 +11,10 @@
 PRIOR_ALPHA = 1e-3
 MESH = pl.DeviceIdType.MESH
 LANE_BLOCK = 512
-N_CHUNKS = 4
+FIRST_TURN = 0
+TURN_AT = 2
+SWAP_SIZES = (1024, 512, 512)
+LATER_SIZES = (1536, 1536, 1024)
 VMEM_LIMIT = 40 * 1024 * 1024
 
 
@@ -44,7 +47,7 @@
     n_z, n_sweeps, log_denom,
     x_hbm, mu_hbm, lp_hbm, beta_hbm,
     mu_out, lp_out, lse_out,
-    x_v, x_t, mu_f, mu_b, p_v, r_v, s_v, s_rx, n_tx, n_rx, c_tx, c_rx,
+    x_v, x_o, x_t, mu_f, mu_b, p_v, r_v, s_v, s_rx, s_rx_end, n_tx, n_rx, c_tx, c_rx,
     z_tx, z_rx, m_v, l_v, sqx_v, lse_v, lse_rx, lp_rx, lp_v, beta_ref,
     ld_sem, xs_sem, xr_sem, zs_sem, zr_sem, ss_sem, sr_sem, ns_sem, nr_sem,
     as_sem, ar_sem, cs_sem, cr_sem, ls_sem, lr_sem, os_sem, or_sem, turn_sem,
@@ -53,9 +56,9 @@
     zz = lax.axis_index("comp")
     core = lax.rem(row, 2)
     yy = lax.div(row, 2)
-    fit = core
-    other = 1 - core
-    y_peer = {"row": (1 - yy) * 2 + core}
+    fit = lax.rem(core + yy, 2)
+    other = 1 - fit
+    y_peer = {"row": (1 - yy) * 2 + (1 - core)}
     c_peer = {"row": yy * 2 + (1 - core)}
     z_peers = [{"comp": lax.rem(zz + d, n_z)} for d in range(1, n_z)]
 
@@ -63,11 +66,16 @@
     own_rows = n_rows // 2
     k_dim, h_dim = mu_f.shape
     k_half = k_dim // 2
-    chunk = n_rows // N_CHUNKS
-    per_chunk = chunk // LANE_BLOCK
     mine = pl.multiple_of(yy * k_half, k_half)
     theirs = pl.multiple_of((1 - yy) * k_half, k_half)
-    own_chunks = N_CHUNKS // 2
+    own_spans = [(i * own_rows // 2, own_rows // 2) for i in range(2)]
+    swap_spans = []
+    for size in SWAP_SIZES:
+        swap_spans.append((sum(SWAP_SIZES[: len(swap_spans)]), size))
+    first_spans = own_spans + [(own_rows + o, size) for o, size in swap_spans]
+    later_spans = []
+    for size in LATER_SIZES:
+        later_spans.append((sum(LATER_SIZES[: len(later_spans)]), size))
     n_col = h_dim // 128
     col_blocks = [slice(g * 128, (g + 1) * 128) for g in range(n_col)]
     lanes = LANE_BLOCK // 128
@@ -86,12 +94,16 @@
     beta_load = pltpu.make_async_copy(beta_hbm, beta_ref, ld_sem.at[0])
     lp_load = pltpu.make_async_copy(lp_hbm, lp_v, ld_sem.at[1])
     mu_load = pltpu.make_async_copy(mu_hbm.at[fit], mu_f, ld_sem.at[2])
+    out_loads = []
+    for i, (o, size) in enumerate(swap_spans):
+        cp = pltpu.make_async_copy(x_hbm.at[pl.ds(o, size), your_cols], x_o.at[pl.ds(o, size)], ld_sem.at[5 + i])
+        cp.start()
+        out_loads.append(cp)
     for cp in (beta_load, lp_load, mu_load):
         cp.start()
     loads = []
-    for i in range(own_chunks):
-        rows = pl.ds(i * chunk, chunk)
-        cp = pltpu.make_async_copy(x_hbm.at[rows, my_cols], x_v.at[rows], ld_sem.at[3 + i])
+    for i, (o, size) in enumerate(own_spans):
+        cp = pltpu.make_async_copy(x_hbm.at[pl.ds(o, size), my_cols], x_v.at[pl.ds(o, size)], ld_sem.at[3 + i])
         cp.start()
         loads.append(cp)
 
@@ -99,11 +111,9 @@
         pl.semaphore_wait(barrier, 1 + n_z)
 
     swaps = []
-    for i in range(own_chunks):
-        cp = remote(
-            x_hbm.at[pl.ds(i * chunk, chunk), your_cols], x_v.at[pl.ds(own_rows + i * chunk, chunk)],
-            xs_sem.at[0], xr_sem.at[i], c_peer,
-        )
+    for i, (o, size) in enumerate(swap_spans):
+        out_loads[i].wait()
+        cp = remote(x_o.at[pl.ds(o, size)], x_v.at[pl.ds(own_rows + o, size)], xs_sem.at[0], xr_sem.at[i], c_peer)
         cp.start()
         swaps.append(cp)
 
@@ -113,7 +123,7 @@
         mu_load.wait()
         mu0 = mu_f[...]
         mu_b[...] = mu0.astype(jnp.bfloat16)
-        lp0 = jnp.where(core == 0, lp_v[0:1, :], lp_v[1:2, :])
+        lp0 = jnp.where(fit == 0, lp_v[0:1, :], lp_v[1:2, :])
         c_row = lp0 - beta_ref[0] * _lane_sum_row(_fold(mu0 * mu0))
         c_col = _col(c_row)
 
@@ -136,16 +146,16 @@
         last = t == n_sweeps - 1
         beta = beta_ref[t]
         par = t % 2
-        for ci in range(N_CHUNKS):
+        spans = first_spans if t == 0 else later_spans
+        for ci, (start, size) in enumerate(spans):
             if t == 0:
                 with jax.named_scope("xwait"):
-                    if ci < own_chunks:
+                    if ci < len(own_spans):
                         loads[ci].wait()
                     else:
-                        swaps[ci - own_chunks].wait_recv()
+                        swaps[ci - len(own_spans)].wait_recv()
             with jax.named_scope("estep"):
-                for bi in range(per_chunk):
-                    r0 = ci * chunk + bi * LANE_BLOCK
+                for r0 in range(start, start + size, LANE_BLOCK):
                     cols = slice(r0, r0 + LANE_BLOCK)
                     if t == 0:
                         a = lax.dot_general(
@@ -157,20 +167,22 @@
                     else:
                         l0 = l_v[:, cols]
                         l1 = softmax_half(half_logits(theirs, c_their_col, beta, cols), 1 - yy, theirs, cols)
-                    z_tx[par, ci, :, bi * LANE_BLOCK : (bi + 1) * LANE_BLOCK] = log_add(l0, l1)
+                    z_tx[par, :, cols] = log_add(l0, l1)
+            span = pl.ds(start, size)
             for d, peer in enumerate(z_peers):
-                remote(z_tx.at[par, ci], z_rx.at[par, ci, d], zs_sem.at[par], zr_sem.at[par, ci], peer).start()
+                remote(
+                    z_tx.at[par, :, span], z_rx.at[par, d, :, span], zs_sem.at[par], zr_sem.at[par, ci], peer
+                ).start()
 
         n_acc = jnp.zeros((k_dim, 128), jnp.float32)
-        for ci in range(N_CHUNKS):
+        for ci, (start, size) in enumerate(spans):
             with jax.named_scope("zwait"):
-                remote(z_rx.at[par, ci], z_rx.at[par, ci], zs_sem.at[par], zr_sem.at[par, ci], z_peers[0]).wait_recv()
+                came = z_rx.at[par, :, :, pl.ds(start, size)]
+                remote(came, came, zs_sem.at[par], zr_sem.at[par, ci], z_peers[0]).wait_recv()
             with jax.named_scope("resp"):
-                for bi in range(per_chunk):
-                    r0 = ci * chunk + bi * LANE_BLOCK
+                for r0 in range(start, start + size, LANE_BLOCK):
                     cols = slice(r0, r0 + LANE_BLOCK)
-                    sl = slice(bi * LANE_BLOCK, (bi + 1) * LANE_BLOCK)
-                    parts = [z_tx[par, ci, :, sl]] + [z_rx[par, ci, d, :, sl] for d in range(n_z - 1)]
+                    parts = [z_tx[par, :, cols]] + [z_rx[par, d, :, cols] for d in range(n_z - 1)]
                     top = functools.reduce(jnp.maximum, parts)
                     tot = functools.reduce(lambda u, v: u + v, [jnp.exp(q - top) for q in parts])
                     lse = top + jnp.log(tot)
@@ -183,7 +195,7 @@
                     n_acc = n_acc + jnp.concatenate(halves, axis=0)
                     if last:
                         lse_v[:, cols] = lse - beta * sqx_v[:, cols]
-                rows = slice(ci * chunk, (ci + 1) * chunk)
+                rows = slice(start, start + size)
                 part = jnp.dot(r_v[pl.ds(theirs, k_half), rows], x_v[rows, :], preferred_element_type=jnp.float32)
                 s_v[pl.ds(theirs, k_half), :] = part if ci == 0 else s_v[pl.ds(theirs, k_half), :] + part
 
@@ -192,16 +204,23 @@
         n_copy = remote(n_tx.at[par], n_rx.at[par], ns_sem.at[0], nr_sem.at[0], y_peer)
         n_copy.start()
 
-        def s_copy(half, g, slot):
+        def arrived(half, g):
+            if g < n_col - 1:
+                return s_rx.at[pl.ds(half, k_half), col_blocks[g]]
+            return s_rx_end.at[par, pl.ds(half, k_half), :]
+
+        def s_copy(half, g, second):
+            end = g == n_col - 1
+            slot = 2 * (n_col - 1) + 2 * par + second if end else second * (n_col - 1) + g
             return remote(
-                s_v.at[pl.ds(half, k_half), col_blocks[g]], s_rx.at[pl.ds(half, k_half), col_blocks[g]],
-                ss_sem.at[0 if g < n_col - 1 else 1], sr_sem.at[slot], y_peer,
+                s_v.at[pl.ds(half, k_half), col_blocks[g]], arrived(half, g),
+                ss_sem.at[1 if end else 0], sr_sem.at[slot], y_peer,
             )
 
-        first_copies = [s_copy(theirs, g, g) for g in range(n_col)]
+        first_copies = [s_copy(theirs, g, 0) for g in range(n_col)]
         s_mine = jax.named_scope("smine")
         early = s_v.at[pl.ds(theirs, k_half), pl.ds(0, h_dim - 128)]
-        late = s_v.at[pl.ds(theirs, k_half), pl.ds(h_dim - 128, 128)]
+        late = s_v.at[:, pl.ds(h_dim - 128, 128)]
         early_sent = remote(early, early, ss_sem.at[0], sr_sem.at[0], y_peer)
         late_sent = remote(late, late, ss_sem.at[1], sr_sem.at[0], y_peer)
 
@@ -209,7 +228,7 @@
             for cp in first_copies:
                 cp.start()
         else:
-            @pl.when(core == 1)
+            @pl.when(fit == FIRST_TURN)
             def _():
                 for cp in first_copies:
                     cp.start()
@@ -218,11 +237,9 @@
             s_v[pl.ds(mine, k_half), :] = jnp.dot(
                 r_v[pl.ds(mine, k_half), :], x_v[...], preferred_element_type=jnp.float32
             )
-        last_copies = []
-        if last:
-            last_copies = [s_copy(mine, g, n_col + g) for g in range(n_col)]
-            for cp in last_copies:
-                cp.start()
+        last_copies = [s_copy(mine, g, 1) for g in (range(n_col) if last else [n_col - 1])]
+        for cp in last_copies:
+            cp.start()
 
         if t == 0:
             with jax.named_scope("xt"):
@@ -230,17 +247,11 @@
                     rows = slice(b * LANE_BLOCK, (b + 1) * LANE_BLOCK)
                     x_t[:, rows] = jnp.transpose(x_v[rows, :])
             with jax.named_scope("turn"):
-                @pl.when(core == 1)
-                def _():
-                    early_sent.wait_send()
-                    pl.semaphore_signal(turn_sem, inc=1, device_id=c_peer, device_id_type=MESH)
-
-                @pl.when(core == 0)
+                @pl.when(fit == 1 - FIRST_TURN)
                 def _():
                     pl.semaphore_wait(turn_sem, 1)
                     for cp in first_copies:
                         cp.start()
-                    early_sent.wait_send()
 
             with jax.named_scope("sqx"):
                 for b in range(n_rows // LANE_BLOCK):
@@ -253,33 +264,51 @@
         n_all = n_part + n_rx[par]
         if not last:
             n_own = jnp.where(yy == 0, n_all[:, 0:k_half], n_all[:, k_half:])
+            n_their = jnp.where(yy == 0, n_all[:, k_half:], n_all[:, 0:k_half])
             inv_col = _col(1.0 / (n_own + EPS_COUNT))
+            inv_their_col = _col(1.0 / (n_their + EPS_COUNT))
+            beta_next = beta_ref[t + 1]
+
+            def new_means(base, g, inv):
+                cols = col_blocks[g]
+                mu = (s_v[pl.ds(base, k_half), cols] + arrived(base, g)[...]) * inv
+                mu_b[pl.ds(base, k_half), cols] = mu.astype(jnp.bfloat16)
+                return mu * mu
+
             sq_acc = jnp.zeros((k_half, 128), jnp.float32)
-            for g, cols in enumerate(col_blocks):
+            for g, cols in enumerate(col_blocks[:-1]):
                 with jax.named_scope("ywait"):
                     first_copies[g].wait_recv()
                 with jax.named_scope("mu"):
-                    mu = (s_v[pl.ds(mine, k_half), cols] + s_rx[pl.ds(mine, k_half), cols]) * inv_col
-                    mu_b[pl.ds(mine, k_half), cols] = mu.astype(jnp.bfloat16)
-                    sq_acc = sq_acc + mu * mu
+                    sq_acc = sq_acc + new_means(mine, g, inv_col)
                 block = mu_b.at[pl.ds(mine, k_half), cols]
                 remote(block, block, as_sem.at[0], ar_sem.at[0], y_peer).start()
-            c_own = jnp.log((n_own + PRIOR_ALPHA) / log_denom) - beta_ref[t + 1] * _lane_sum_row(sq_acc)
-            c_tx[par] = c_own
+                if t == 0 and g == TURN_AT:
+                    @pl.when(fit == FIRST_TURN)
+                    def _():
+                        pl.semaphore_signal(turn_sem, inc=1, device_id=c_peer, device_id_type=MESH)
+            c_part = jnp.log((n_own + PRIOR_ALPHA) / log_denom) - beta_next * _lane_sum_row(sq_acc)
+            c_tx[par] = c_part
             c_copy = remote(c_tx.at[par], c_rx.at[par], cs_sem.at[0], cr_sem.at[0], y_peer)
             c_copy.start()
+            with jax.named_scope("ywait"):
+                first_copies[-1].wait_recv()
+            c_own = c_part - beta_next * _lane_sum_row(new_means(mine, n_col - 1, inv_col))
             c_own_col = _col(c_own)
             with jax.named_scope("emine"):
                 for b in range(n_rows // LANE_BLOCK):
                     cols = slice(b * LANE_BLOCK, (b + 1) * LANE_BLOCK)
                     l_v[:, cols] = softmax_half(
-                        half_logits(mine, c_own_col, beta_ref[t + 1], cols), yy, mine, cols
+                        half_logits(mine, c_own_col, beta_next, cols), yy, mine, cols
                     )
             with jax.named_scope("cwait"):
+                last_copies[0].wait_recv()
+                sq_their = _lane_sum_row(new_means(theirs, n_col - 1, inv_their_col))
                 c_copy.wait_recv()
-                c_their_col = _col(c_rx[par])
+                c_their_col = _col(c_rx[par] - beta_next * sq_their)
             with jax.named_scope("muwait"):
-                sent, came = mu_b.at[pl.ds(mine, k_half)], mu_b.at[pl.ds(theirs, k_half)]
+                rest = pl.ds(0, h_dim - 128)
+                sent, came = mu_b.at[pl.ds(mine, k_half), rest], mu_b.at[pl.ds(theirs, k_half), rest]
                 remote(sent, came, as_sem.at[0], ar_sem.at[0], y_peer).wait()
                 c_copy.wait_send()
         else:
@@ -290,13 +319,6 @@
             lp_copy = remote(n_tx.at[1 - par], lp_rx, ls_sem.at[1], lr_sem.at[1], c_peer)
             lp_copy.start()
             inv_col = _col(1.0 / (n_all + EPS_COUNT))
-            lse_copy.wait_recv()
-            own_lse = lse_v[:, 0:own_rows]
-            lse_out[0:1, :] = jnp.where(core == 0, own_lse, lse_rx[...])
-            lse_out[1:2, :] = jnp.where(core == 0, lse_rx[...], own_lse)
-            lp_copy.wait_recv()
-            lp_out[0:1, :] = jnp.where(core == 0, lp_row, lp_rx[...])
-            lp_out[1:2, :] = jnp.where(core == 0, lp_rx[...], lp_row)
             for half in range(2):
                 base = mine if half == 0 else theirs
                 inv_half = jnp.where(yy == half, inv_col[0:k_half, :], inv_col[k_half:, :])
@@ -305,10 +327,17 @@
                         (first_copies if half == 0 else last_copies)[g].wait_recv()
                     with jax.named_scope("fmu"):
                         mu_out[fit, pl.ds(base, k_half), cols] = (
-                            s_v[pl.ds(base, k_half), cols] + s_rx[pl.ds(base, k_half), cols]
+                            s_v[pl.ds(base, k_half), cols] + arrived(base, g)[...]
                         ) * inv_half
                     block = mu_out.at[fit, pl.ds(base, k_half), cols]
                     remote(block, block, os_sem.at[0], or_sem.at[0], c_peer).start()
+            lse_copy.wait_recv()
+            own_lse = lse_v[:, 0:own_rows]
+            lse_out[0:1, :] = jnp.where(fit == 0, own_lse, lse_rx[...])
+            lse_out[1:2, :] = jnp.where(fit == 0, lse_rx[...], own_lse)
+            lp_copy.wait_recv()
+            lp_out[0:1, :] = jnp.where(fit == 0, lp_row, lp_rx[...])
+            lp_out[1:2, :] = jnp.where(fit == 0, lp_rx[...], lp_row)
             lse_copy.wait_send()
             lp_copy.wait_send()
             with jax.named_scope("owait"):
@@ -321,8 +350,7 @@
                 both = s_v.at[:, pl.ds(h_dim - 128, 128)]
                 remote(both, both, ss_sem.at[1], sr_sem.at[0], y_peer).wait_send()
             else:
-                if t > 0:
-                    early_sent.wait_send()
+                early_sent.wait_send()
                 late_sent.wait_send()
             remote(z_rx.at[par], z_rx.at[par], zs_sem.at[par], zr_sem.at[par, 0], z_peers[0]).wait_send()
     sent = x_v.at[pl.ds(own_rows, own_rows)]
@@ -356,7 +384,6 @@
         _, k_dim, h_dim = mu_init.shape
         n_sweeps = inv_temp.shape[0]
         total = 2 * n_rows
-        chunk = total // N_CHUNKS
         k_half = k_dim // 2
         col_blocks = h_dim // 128
         log_denom = float(n_rows * row_size + k_dim * n_z * PRIOR_ALPHA)
@@ -378,19 +405,21 @@
             ),
             scratch_shapes=[
                 pltpu.VMEM((total, h_dim), bf16),
+                pltpu.VMEM((n_rows, h_dim), bf16),
                 pltpu.VMEM((h_dim, total), bf16),
                 pltpu.VMEM((k_dim, h_dim), f32),
                 pltpu.VMEM((k_dim, h_dim), bf16),
                 pltpu.VMEM((k_dim, total), f32),
                 pltpu.VMEM((k_dim, total), bf16),
                 pltpu.VMEM((k_dim, h_dim), f32),
-                pltpu.VMEM((k_dim, h_dim), f32),
+                pltpu.VMEM((k_dim, h_dim - 128), f32),
+                pltpu.VMEM((2, k_dim, 128), f32),
                 pltpu.VMEM((2, 1, k_dim), f32),
                 pltpu.VMEM((2, 1, k_dim), f32),
                 pltpu.VMEM((2, 1, k_half), f32),
                 pltpu.VMEM((2, 1, k_half), f32),
-                pltpu.VMEM((2, N_CHUNKS, 1, chunk), f32),
-                pltpu.VMEM((2, N_CHUNKS, n_z - 1, 1, chunk), f32),
+                pltpu.VMEM((2, 1, total), f32),
+                pltpu.VMEM((2, n_z - 1, 1, total), f32),
                 pltpu.VMEM((2, 1, total), f32),
                 pltpu.VMEM((1, total), f32),
                 pltpu.VMEM((1, total), f32),
@@ -399,10 +428,10 @@
                 pltpu.VMEM((1, k_dim), f32),
                 pltpu.VMEM((2, k_dim), f32),
                 pltpu.SMEM((n_sweeps,), f32),
-                dma((3 + N_CHUNKS // 2,)),
-                dma((1,)), dma((N_CHUNKS // 2,)),
-                dma((2,)), dma((2, N_CHUNKS)),
-                dma((2,)), dma((2 * col_blocks,)),
+                dma((5 + len(SWAP_SIZES),)),
+                dma((1,)), dma((len(SWAP_SIZES),)),
+                dma((2,)), dma((2, max(2 + len(SWAP_SIZES), len(LATER_SIZES)))),
+                dma((2,)), dma((2 * col_blocks + 2,)),
                 dma((1,)), dma((1,)),
                 dma((1,)), dma((1,)),
                 dma((1,)), dma((1,)),

time: 56 us -> 54.8 us (0.979)
  Pallas kernels: 55.1 us -> 53.8 us
    pallas_call x1, Pallas kernels: 54 us -> 52.8 us  [local_fit(): pl.pallas_call(functools.partial(em_kernel, n_z, n_sweeps, log_denom), ou...]
where the time goes in v4:
time: 54.8 us; the launch traced here: 54.6 us
  Pallas kernels  53.8 us (98%)
  between operations  0.8 us (1%)
    pallas_call x1, Pallas kernels, local_fit(): pl.pallas_call(functools.partial(em_kernel, n_z, n_sweeps, log_denom), ou...  52.8 us

profile of v4, /device:TPU:0, one launch (start us, length us, event | category | flops | bytes accessed | tf_op | source)
XLA Modules:
  0.0 54.6 jit_solution(15868052884094714296)
XLA Ops:
  0.6 52.8 %em_kernel.1 = (f32[2,256,512]{2,1,0:T(8,128)S(1)}, f32[2,256]{1,0:T(2,128)S(1)}, f32[2,2048]{1,0:T(2,128)S(1)}) custom-call(bf16[2048,1024]{1,0:T(8,128)(2,1)} %x_hbm.1, f32[2,256,512]{2,1,0:T(8,128)} %mu_hbm.1, f32[2,256]{1,0:T(2,128)} %lp_hbm.1, f32[3]{0:T(128)} %beta_hbm.1), custom_call_target="tpu_custom_call" | custom-call | tf_op jit(solution)/shard_map/em_kernel/pallas_call | solution.py:393
  53.4 1.1 %store_kernel.1 = (f32[2,256,512]{2,1,0:T(8,128)}, f32[2,256]{1,0:T(2,128)}, f32[2,2048]{1,0:T(2,128)}) custom-call(f32[2,256,512]{2,1,0:T(8,128)S(1)} %get-tuple-element.6.mu_ref, f32[2,256]{1,0:T(2,128)S(1)} %get-tuple-element.7.lp_ref, f32[2,2048]{1,0:T(2,128)S(1)} %get-tuple-element.8.lse_ref), custom_call_target="tpu_custom_call" | custom-call | tf_op jit(solution)/shard_map/store_kernel/pallas_call | solution.py:447

commit v5 on v4

--- a/solution.py
+++ b/solution.py
@@ -13,6 +13,7 @@
 LANE_BLOCK = 512
 FIRST_TURN = 0
 TURN_AT = 2
+OWN_SPLIT = 3072
 SWAP_SIZES = (1024, 512, 512)
 LATER_SIZES = (1536, 1536, 1024)
 VMEM_LIMIT = 40 * 1024 * 1024
@@ -47,10 +48,10 @@
     n_z, n_sweeps, log_denom,
     x_hbm, mu_hbm, lp_hbm, beta_hbm,
     mu_out, lp_out, lse_out,
-    x_v, x_o, x_t, mu_f, mu_b, p_v, r_v, s_v, s_rx, s_rx_end, n_tx, n_rx, c_tx, c_rx,
+    x_v, x_t, mu_f, mu_b, p_v, r_v, s_v, s_rx, s_rx_end, n_tx, n_rx, c_tx, c_rx,
     z_tx, z_rx, m_v, l_v, sqx_v, lse_v, lse_rx, lp_rx, lp_v, beta_ref,
     ld_sem, xs_sem, xr_sem, zs_sem, zr_sem, ss_sem, sr_sem, ns_sem, nr_sem,
-    as_sem, ar_sem, cs_sem, cr_sem, ls_sem, lr_sem, os_sem, or_sem, turn_sem,
+    as_sem, ar_sem, cs_sem, cr_sem, ls_sem, lr_sem, os_sem, or_sem, turn_sem, here_sem, all_sem,
 ):
     row = lax.axis_index("row")
     zz = lax.axis_index("comp")
@@ -60,7 +61,10 @@
     other = 1 - fit
     y_peer = {"row": (1 - yy) * 2 + (1 - core)}
     c_peer = {"row": yy * 2 + (1 - core)}
-    z_peers = [{"comp": lax.rem(zz + d, n_z)} for d in range(1, n_z)]
+    far, near = 3 * ((3 - zz) // 2), 1 + zz % 2
+    z_index = [far, 6 - zz - far - near, near]
+    z_peers = [{"comp": z} for z in z_index]
+    z_slots = [lax.rem(z - zz + n_z, n_z) - 1 for z in z_index]
 
     n_rows = x_v.shape[0]
     own_rows = n_rows // 2
@@ -86,19 +90,19 @@
         )
 
     barrier = pltpu.get_barrier_semaphore()
-    for peer in [c_peer, y_peer] + z_peers:
-        pl.semaphore_signal(barrier, inc=1, device_id=peer, device_id_type=MESH)
+
+    def signal(sem, peer):
+        pl.semaphore_signal(sem, inc=1, device_id=peer, device_id_type=MESH)
+
+    @pl.when(core == 1)
+    def _():
+        signal(barrier, c_peer)
 
     my_cols = pl.ds(pl.multiple_of(fit * h_dim, h_dim), h_dim)
     your_cols = pl.ds(pl.multiple_of(other * h_dim, h_dim), h_dim)
     beta_load = pltpu.make_async_copy(beta_hbm, beta_ref, ld_sem.at[0])
     lp_load = pltpu.make_async_copy(lp_hbm, lp_v, ld_sem.at[1])
     mu_load = pltpu.make_async_copy(mu_hbm.at[fit], mu_f, ld_sem.at[2])
-    out_loads = []
-    for i, (o, size) in enumerate(swap_spans):
-        cp = pltpu.make_async_copy(x_hbm.at[pl.ds(o, size), your_cols], x_o.at[pl.ds(o, size)], ld_sem.at[5 + i])
-        cp.start()
-        out_loads.append(cp)
     for cp in (beta_load, lp_load, mu_load):
         cp.start()
     loads = []
@@ -108,12 +112,20 @@
         loads.append(cp)
 
     with jax.named_scope("enter"):
-        pl.semaphore_wait(barrier, 1 + n_z)
+        @pl.when(core == 0)
+        def _():
+            pl.semaphore_wait(barrier, 1)
+            signal(here_sem, c_peer)
+
+        @pl.when(core == 1)
+        def _():
+            pl.semaphore_wait(here_sem, 1)
+            for peer in [{"row": (1 - yy) * 2 + 1}] + z_peers:
+                signal(barrier, peer)
 
     swaps = []
     for i, (o, size) in enumerate(swap_spans):
-        out_loads[i].wait()
-        cp = remote(x_o.at[pl.ds(o, size)], x_v.at[pl.ds(own_rows + o, size)], xs_sem.at[0], xr_sem.at[i], c_peer)
+        cp = remote(x_hbm.at[pl.ds(o, size), your_cols], x_v.at[pl.ds(own_rows + o, size)], xs_sem.at[0], xr_sem.at[i], c_peer)
         cp.start()
         swaps.append(cp)
 
@@ -168,10 +180,21 @@
                         l0 = l_v[:, cols]
                         l1 = softmax_half(half_logits(theirs, c_their_col, beta, cols), 1 - yy, theirs, cols)
                     z_tx[par, :, cols] = log_add(l0, l1)
+            if t == 0 and ci == 0:
+                with jax.named_scope("peers"):
+                    @pl.when(core == 1)
+                    def _():
+                        pl.semaphore_wait(barrier, n_z)
+                        signal(all_sem, c_peer)
+
+                    @pl.when(core == 0)
+                    def _():
+                        pl.semaphore_wait(all_sem, 1)
+
             span = pl.ds(start, size)
-            for d, peer in enumerate(z_peers):
+            for slot, peer in zip(z_slots, z_peers):
                 remote(
-                    z_tx.at[par, :, span], z_rx.at[par, d, :, span], zs_sem.at[par], zr_sem.at[par, ci], peer
+                    z_tx.at[par, :, span], z_rx.at[par, slot, :, span], zs_sem.at[par], zr_sem.at[par, ci], peer
                 ).start()
 
         n_acc = jnp.zeros((k_dim, 128), jnp.float32)
@@ -295,17 +318,21 @@
                 first_copies[-1].wait_recv()
             c_own = c_part - beta_next * _lane_sum_row(new_means(mine, n_col - 1, inv_col))
             c_own_col = _col(c_own)
+            def own_logits(lo, hi):
+                for r0 in range(lo, hi, LANE_BLOCK):
+                    cols = slice(r0, r0 + LANE_BLOCK)
+                    l_v[:, cols] = softmax_half(half_logits(mine, c_own_col, beta_next, cols), yy, mine, cols)
+
             with jax.named_scope("emine"):
-                for b in range(n_rows // LANE_BLOCK):
-                    cols = slice(b * LANE_BLOCK, (b + 1) * LANE_BLOCK)
-                    l_v[:, cols] = softmax_half(
-                        half_logits(mine, c_own_col, beta_next, cols), yy, mine, cols
-                    )
+                own_logits(0, OWN_SPLIT)
+            with jax.named_scope("bwait"):
+                last_copies[0].wait_recv()
+            with jax.named_scope("emine"):
+                sq_their = beta_next * _lane_sum_row(new_means(theirs, n_col - 1, inv_their_col))
+                own_logits(OWN_SPLIT, n_rows)
             with jax.named_scope("cwait"):
-                last_copies[0].wait_recv()
-                sq_their = _lane_sum_row(new_means(theirs, n_col - 1, inv_their_col))
                 c_copy.wait_recv()
-                c_their_col = _col(c_rx[par] - beta_next * sq_their)
+                c_their_col = _col(c_rx[par] - sq_their)
             with jax.named_scope("muwait"):
                 rest = pl.ds(0, h_dim - 128)
                 sent, came = mu_b.at[pl.ds(mine, k_half), rest], mu_b.at[pl.ds(theirs, k_half), rest]
@@ -405,7 +432,6 @@
             ),
             scratch_shapes=[
                 pltpu.VMEM((total, h_dim), bf16),
-                pltpu.VMEM((n_rows, h_dim), bf16),
                 pltpu.VMEM((h_dim, total), bf16),
                 pltpu.VMEM((k_dim, h_dim), f32),
                 pltpu.VMEM((k_dim, h_dim), bf16),
@@ -428,7 +454,7 @@
                 pltpu.VMEM((1, k_dim), f32),
                 pltpu.VMEM((2, k_dim), f32),
                 pltpu.SMEM((n_sweeps,), f32),
-                dma((5 + len(SWAP_SIZES),)),
+                dma((5,)),
                 dma((1,)), dma((len(SWAP_SIZES),)),
                 dma((2,)), dma((2, max(2 + len(SWAP_SIZES), len(LATER_SIZES)))),
                 dma((2,)), dma((2 * col_blocks + 2,)),
@@ -437,6 +463,8 @@
                 dma((1,)), dma((1,)),
                 dma((2,)), dma((2,)),
                 dma((1,)), dma((1,)),
+                pltpu.SemaphoreType.REGULAR,
+                pltpu.SemaphoreType.REGULAR,
                 pltpu.SemaphoreType.REGULAR,
             ],
             compiler_params=pltpu.CompilerParams(

time: 54.8 us -> 53.5 us (0.976)
  Pallas kernels: 53.8 us -> 52.6 us
    pallas_call x1, Pallas kernels: 52.8 us -> 51.5 us  [local_fit(): pl.pallas_call(functools.partial(em_kernel, n_z, n_sweeps, log_denom), ou...]
where the time goes in v5:
time: 53.5 us; the launch traced here: 53.4 us
  Pallas kernels  52.6 us (98%)
  between operations  0.8 us (1%)
    pallas_call x1, Pallas kernels, local_fit(): pl.pallas_call(functools.partial(em_kernel, n_z, n_sweeps, log_denom), ou...  51.5 us

profile of v5, /device:TPU:0, one launch (start us, length us, event | category | flops | bytes accessed | tf_op | source)
XLA Modules:
  0.0 53.4 jit_solution(3427375320630673675)
XLA Ops:
  0.6 51.5 %em_kernel.1 = (f32[2,256,512]{2,1,0:T(8,128)S(1)}, f32[2,256]{1,0:T(2,128)S(1)}, f32[2,2048]{1,0:T(2,128)S(1)}) custom-call(bf16[2048,1024]{1,0:T(8,128)(2,1)} %x_hbm.1, f32[2,256,512]{2,1,0:T(8,128)} %mu_hbm.1, f32[2,256]{1,0:T(2,128)} %lp_hbm.1, f32[3]{0:T(128)} %beta_hbm.1), custom_call_target="tpu_custom_call" | custom-call | tf_op jit(solution)/shard_map/em_kernel/pallas_call | solution.py:420
  52.2 1.1 %store_kernel.1 = (f32[2,256,512]{2,1,0:T(8,128)}, f32[2,256]{1,0:T(2,128)}, f32[2,2048]{1,0:T(2,128)}) custom-call(f32[2,256,512]{2,1,0:T(8,128)S(1)} %get-tuple-element.6.mu_ref, f32[2,256]{1,0:T(2,128)S(1)} %get-tuple-element.7.lp_ref, f32[2,2048]{1,0:T(2,128)S(1)} %get-tuple-element.8.lse_ref), custom_call_target="tpu_custom_call" | custom-call | tf_op jit(solution)/shard_map/store_kernel/pallas_call | solution.py:475

commit v6 on v5

--- a/solution.py
+++ b/solution.py
@@ -151,7 +151,8 @@
         return top + jnp.log(jnp.exp(u - top) + jnp.exp(v - top))
 
     def half_logits(base, cc, beta, cols):
-        a = jnp.dot(mu_b[pl.ds(base, k_half), :], x_t[:, cols], preferred_element_type=jnp.float32)
+        points = jnp.concatenate([x_t[j] for j in range(cols.start // 128, cols.stop // 128)], axis=1)
+        a = jnp.dot(mu_b[pl.ds(base, k_half), :], points, preferred_element_type=jnp.float32)
         return a * (2.0 * beta) + jnp.concatenate([cc] * lanes, axis=1)
 
     for t in range(n_sweeps):
@@ -268,7 +269,9 @@
             with jax.named_scope("xt"):
                 for b in range(n_rows // LANE_BLOCK):
                     rows = slice(b * LANE_BLOCK, (b + 1) * LANE_BLOCK)
-                    x_t[:, rows] = jnp.transpose(x_v[rows, :])
+                    turned = jnp.transpose(x_v[rows, :])
+                    for j in range(lanes):
+                        x_t[b * lanes + j] = turned[:, j * 128 : (j + 1) * 128]
             with jax.named_scope("turn"):
                 @pl.when(fit == 1 - FIRST_TURN)
                 def _():
@@ -277,10 +280,9 @@
                         cp.start()
 
             with jax.named_scope("sqx"):
-                for b in range(n_rows // LANE_BLOCK):
-                    cols = slice(b * LANE_BLOCK, (b + 1) * LANE_BLOCK)
-                    xf = x_t[:, cols].astype(jnp.float32)
-                    sqx_v[:, cols] = jnp.sum(xf * xf, axis=0, keepdims=True)
+                for j in range(n_rows // 128):
+                    xf = x_t[j].astype(jnp.float32)
+                    sqx_v[:, j * 128 : (j + 1) * 128] = jnp.sum(xf * xf, axis=0, keepdims=True)
 
         with jax.named_scope("nwait"):
             n_copy.wait_recv()
@@ -386,7 +388,7 @@
 
 def store_kernel(mu_ref, lp_ref, lse_ref, mu_out, lp_out, lse_out, sems):
     copies = []
-    parts = 4
+    parts = 1
     step = mu_ref.shape[1] // parts
     for s in range(mu_ref.shape[0]):
         for i in range(parts):
@@ -432,7 +434,7 @@
             ),
             scratch_shapes=[
                 pltpu.VMEM((total, h_dim), bf16),
-                pltpu.VMEM((h_dim, total), bf16),
+                pltpu.VMEM((total // 128, h_dim, 128), bf16),
                 pltpu.VMEM((k_dim, h_dim), f32),
                 pltpu.VMEM((k_dim, h_dim), bf16),
                 pltpu.VMEM((k_dim, total), f32),
@@ -481,7 +483,7 @@
             ),
             in_specs=[pl.BlockSpec(memory_space=pltpu.VMEM)] * 3,
             out_specs=(pl.BlockSpec(memory_space=pl.ANY),) * 3,
-            scratch_shapes=[dma((2 + 2 * 4,))],
+            scratch_shapes=[dma((2 + 2 * 1,))],
             compiler_params=pltpu.CompilerParams(vmem_limit_bytes=4 * 1024 * 1024),
             name="store_kernel",
         )(mu, lp, lse)

time: 53.5 us -> 53.5 us (level)
  no operation moved by 1% of the time
where the time goes in v6:
time: 53.5 us; the launch traced here: 53.3 us
  Pallas kernels  52.5 us (98%)
  between operations  0.8 us (1%)
    pallas_call x1, Pallas kernels, local_fit(): pl.pallas_call(functools.partial(em_kernel, n_z, n_sweeps, log_denom), ou...  51.5 us

profile of v6, /device:TPU:0, one launch (start us, length us, event | category | flops | bytes accessed | tf_op | source)
XLA Modules:
  0.0 53.3 jit_solution(5992798086285791912)
XLA Ops:
  0.6 51.5 %em_kernel.1 = (f32[2,256,512]{2,1,0:T(8,128)S(1)}, f32[2,256]{1,0:T(2,128)S(1)}, f32[2,2048]{1,0:T(2,128)S(1)}) custom-call(bf16[2048,1024]{1,0:T(8,128)(2,1)} %x_hbm.1, f32[2,256,512]{2,1,0:T(8,128)} %mu_hbm.1, f32[2,256]{1,0:T(2,128)} %lp_hbm.1, f32[3]{0:T(128)} %beta_hbm.1), custom_call_target="tpu_custom_call" | custom-call | tf_op jit(solution)/shard_map/em_kernel/pallas_call | solution.py:422
  52.2 1.0 %store_kernel.1 = (f32[2,256,512]{2,1,0:T(8,128)}, f32[2,256]{1,0:T(2,128)}, f32[2,2048]{1,0:T(2,128)}) custom-call(f32[2,256,512]{2,1,0:T(8,128)S(1)} %get-tuple-element.6.mu_ref, f32[2,256]{1,0:T(2,128)S(1)} %get-tuple-element.7.lp_ref, f32[2,2048]{1,0:T(2,128)S(1)} %get-tuple-element.8.lse_ref), custom_call_target="tpu_custom_call" | custom-call | tf_op jit(solution)/shard_map/store_kernel/pallas_call | solution.py:477

commit v7 on v6

--- a/solution.py
+++ b/solution.py
@@ -195,14 +195,14 @@
             span = pl.ds(start, size)
             for slot, peer in zip(z_slots, z_peers):
                 remote(
-                    z_tx.at[par, :, span], z_rx.at[par, slot, :, span], zs_sem.at[par], zr_sem.at[par, ci], peer
+                    z_tx.at[par, :, span], z_rx.at[par, slot, :, span], zs_sem.at[par], zr_sem.at[par * len(first_spans) + ci], peer
                 ).start()
 
         n_acc = jnp.zeros((k_dim, 128), jnp.float32)
         for ci, (start, size) in enumerate(spans):
             with jax.named_scope("zwait"):
                 came = z_rx.at[par, :, :, pl.ds(start, size)]
-                remote(came, came, zs_sem.at[par], zr_sem.at[par, ci], z_peers[0]).wait_recv()
+                remote(came, came, zs_sem.at[par], zr_sem.at[par * len(first_spans) + ci], z_peers[0]).wait_recv()
             with jax.named_scope("resp"):
                 for r0 in range(start, start + size, LANE_BLOCK):
                     cols = slice(r0, r0 + LANE_BLOCK)
@@ -381,7 +381,7 @@
             else:
                 early_sent.wait_send()
                 late_sent.wait_send()
-            remote(z_rx.at[par], z_rx.at[par], zs_sem.at[par], zr_sem.at[par, 0], z_peers[0]).wait_send()
+            remote(z_rx.at[par], z_rx.at[par], zs_sem.at[par], zr_sem.at[0], z_peers[0]).wait_send()
     sent = x_v.at[pl.ds(own_rows, own_rows)]
     remote(sent, sent, xs_sem.at[0], xr_sem.at[0], c_peer).wait_send()
 
@@ -458,7 +458,7 @@
                 pltpu.SMEM((n_sweeps,), f32),
                 dma((5,)),
                 dma((1,)), dma((len(SWAP_SIZES),)),
-                dma((2,)), dma((2, max(2 + len(SWAP_SIZES), len(LATER_SIZES)))),
+                dma((2,)), dma((2 + len(SWAP_SIZES) + len(LATER_SIZES),)),
                 dma((2,)), dma((2 * col_blocks + 2,)),
                 dma((1,)), dma((1,)),
                 dma((1,)), dma((1,)),

time: 53.5 us -> 53.5 us (level)
  no operation moved by 1% of the time
where the time goes in v7:
time: 53.5 us; the launch traced here: 53.3 us
  Pallas kernels  52.5 us (98%)
  between operations  0.8 us (1%)
    pallas_call x1, Pallas kernels, local_fit(): pl.pallas_call(functools.partial(em_kernel, n_z, n_sweeps, log_denom), ou...  51.5 us

profile of v7, /device:TPU:0, one launch (start us, length us, event | category | flops | bytes accessed | tf_op | source)
XLA Modules:
  0.0 53.3 jit_solution(16233962970068054793)
XLA Ops:
  0.6 51.5 %em_kernel.1 = (f32[2,256,512]{2,1,0:T(8,128)S(1)}, f32[2,256]{1,0:T(2,128)S(1)}, f32[2,2048]{1,0:T(2,128)S(1)}) custom-call(bf16[2048,1024]{1,0:T(8,128)(2,1)} %x_hbm.1, f32[2,256,512]{2,1,0:T(8,128)} %mu_hbm.1, f32[2,256]{1,0:T(2,128)} %lp_hbm.1, f32[3]{0:T(128)} %beta_hbm.1), custom_call_target="tpu_custom_call" | custom-call | tf_op jit(solution)/shard_map/em_kernel/pallas_call | solution.py:422
  52.1 1.0 %store_kernel.1 = (f32[2,256,512]{2,1,0:T(8,128)}, f32[2,256]{1,0:T(2,128)}, f32[2,2048]{1,0:T(2,128)}) custom-call(f32[2,256,512]{2,1,0:T(8,128)S(1)} %get-tuple-element.6.mu_ref, f32[2,256]{1,0:T(2,128)S(1)} %get-tuple-element.7.lp_ref, f32[2,2048]{1,0:T(2,128)S(1)} %get-tuple-element.8.lse_ref), custom_call_target="tpu_custom_call" | custom-call | tf_op jit(solution)/shard_map/store_kernel/pallas_call | solution.py:477
